TPU v7x, 128 devices: a whole 4x4x4 slice. The times are simulated.
128 devices in a mesh: dp: 8 (over x, z_lo), vocab: 16 (over z_hi, y, core).
Axes of the slice: x: 4, y: 4, z: 4 (z_hi: 2, z_lo: 2; z = z_hi * 2 + z_lo), core: 2. Of those that a mesh axis runs over, the one named last changes fastest.
Arguments:
- hidden: bfloat16 [1024, 2048], P('dp'), may hold values from -6 to 6
- mix_weight: bfloat16 [2048, 4], replicated, may hold values from -0.125 to 0.125
- proj_weight: bfloat16 [4, 2048, 2048], P(None, None, 'vocab'), may hold values from -0.125 to 0.125
- out_weight: bfloat16 [2048, 65536], P(None, 'vocab'), may hold values from -0.15625 to 0.15625
- saved_lse: float32 [1024, 4], P('dp'), may hold values from 1 to 30
- targets: int32 [1024], P('dp'), may hold values from 0 to 65535
- loss_scale: float32 [1024], P('dp'), may hold values from 4 to 32
Outputs:
- grad_hidden: bfloat16 [1024, 2048], P('dp', 'vocab')
- grad_mix: float32 [2048, 4], P('dp')
- grad_proj: bfloat16 [4, 2048, 2048], P(None, 'dp', 'vocab')
- grad_out: bfloat16 [2048, 65536], P('dp', 'vocab')
All inputs are finite; a program needn't handle non-finite values.
Results may differ from a plain program's by a relative error of at most 0.023.
Values may be sent and summed in bfloat16 or wider, within the bound.
A program may use at most 128 MiB of HBM per device.

v0:
```python
import jax
import jax.numpy as jnp
from jax import lax
from jax.sharding import Mesh
from jax.sharding import PartitionSpec as P

DP = ("dp_0", "dp_1")


def from_everyone(array, axis):
    copies = jnp.broadcast_to(array, (lax.axis_size(axis), *array.shape))
    return lax.all_to_all(copies, axis, split_axis=0, concat_axis=0, tiled=True)


def taken_together(array, axis):
    everything = from_everyone(array, axis)
    return jnp.sum(everything, axis=0)


def sum_by_axis(terms, axes):
    subtotal = terms.astype(jnp.bfloat16)
    for axis in axes:
        subtotal = lax.psum_scatter(subtotal, axis, scatter_dimension=0, tiled=True)
    return subtotal.astype(jnp.float32)


def in_blocks(array, dim, count):
    shape = array.shape
    parts = array.reshape(*shape[:dim], count, shape[dim] // count, *shape[dim + 1 :])
    return jnp.moveaxis(parts, dim, 0)


def sum_at_owner(array, axis, dim):
    count = lax.axis_size(axis)
    parts = lax.all_to_all(in_blocks(array, dim, count), axis, 0, 0, tiled=True)
    return jnp.sum(parts.astype(jnp.float32), axis=0)


def shards(hidden, mix_weight, proj_weight, out_weight, saved_lse, targets, loss_scale):
    token_count = hidden.shape[0]
    model_width = hidden.shape[1]
    comp_count = proj_weight.shape[0]
    col_count = proj_weight.shape[2]
    vocab_local = out_weight.shape[1]
    vocab_index = lax.axis_index("vocab")
    block_rows = token_count * comp_count
    mix_logits = jnp.dot(hidden, mix_weight, preferred_element_type=jnp.float32)
    log_mix = mix_logits - jnp.log(jnp.sum(jnp.exp(mix_logits), axis=1, keepdims=True))
    mix_prob = jnp.exp(log_mix)
    pre_local = jnp.einsum("td,kde->tke", hidden, proj_weight, preferred_element_type=jnp.float32)
    comp_local = jnp.tanh(pre_local).astype(jnp.bfloat16)
    comp_all = lax.all_gather(comp_local, "vocab", axis=2, tiled=True)
    comp_rows = comp_all.reshape(block_rows, model_width)
    logits = jnp.dot(comp_rows, out_weight, preferred_element_type=jnp.float32)
    lse_flat = saved_lse.reshape(block_rows)
    probabilities = jnp.exp(logits - lse_flat[:, None])
    target_rows = jnp.broadcast_to(targets[:, None], (token_count, comp_count)).reshape(block_rows)
    local_target = target_rows - vocab_index * vocab_local
    onehot = lax.broadcasted_iota(jnp.int32, (1, vocab_local), 1) == local_target[:, None]
    target_part = jnp.sum(jnp.where(onehot, logits, 0.0), axis=1)
    target_logit = taken_together(target_part.reshape(token_count, comp_count), "vocab")
    weights = jnp.exp(log_mix + target_logit - saved_lse)
    responsibility = weights / jnp.sum(weights, axis=1, keepdims=True)
    coefficient = (loss_scale[:, None] * responsibility).reshape(block_rows)
    grad_logits = (coefficient[:, None] * (probabilities - onehot.astype(jnp.float32))).astype(
        jnp.bfloat16
    )
    grad_mix_logit = -loss_scale[:, None] * (responsibility - mix_prob)
    part_rows = out_weight
    local_grad = lax.psum_scatter(
        lax.dot_general(
            part_rows, grad_logits, (((1,), (1,)), ((), ())), preferred_element_type=jnp.float32
        ).astype(jnp.bfloat16),
        "vocab",
        scatter_dimension=0,
        tiled=True,
    ).astype(jnp.float32)
    part_rows = comp_rows
    summed = sum_by_axis(
        lax.dot_general(
            part_rows, grad_logits, (((0,), (0,)), ((), ())), preferred_element_type=jnp.float32
        ),
        DP,
    )
    grad_out = summed.astype(jnp.bfloat16)
    comp_float = comp_local.astype(jnp.float32)
    grad_pre = (
        local_grad.T.reshape(token_count, comp_count, col_count) * (1.0 - comp_float * comp_float)
    ).astype(jnp.bfloat16)
    proj_term = jnp.einsum("td,tke->kde", hidden, grad_pre, preferred_element_type=jnp.float32)
    mix_term = jnp.dot(
        hidden.astype(jnp.float32).T, grad_mix_logit, precision=lax.Precision.HIGHEST
    )
    proj_sum, mix_sum = (
        sum_at_owner(proj_term.astype(jnp.bfloat16), DP, 1),
        sum_at_owner(mix_term.astype(jnp.bfloat16), DP, 0),
    )
    hidden_term = jnp.einsum(
        "tke,kde->td", grad_pre, proj_weight, preferred_element_type=jnp.float32
    )
    hidden_part = sum_at_owner(hidden_term.astype(jnp.bfloat16), "vocab", 1)
    mix_rows = lax.dynamic_slice_in_dim(mix_weight, vocab_index * col_count, col_count, 0).astype(
        jnp.float32
    )
    grad_hidden = (
        hidden_part + jnp.dot(grad_mix_logit, mix_rows.T, precision=lax.Precision.HIGHEST)
    ).astype(jnp.bfloat16)
    return (grad_hidden, mix_sum, proj_sum.astype(jnp.bfloat16), grad_out)


def solution(mesh):
    finer = Mesh(mesh.devices.reshape(4, 2, mesh.shape["vocab"]), ("dp_0", "dp_1", "vocab"))
    in_specs = (
        P(DP, None),
        P(),
        P(None, None, "vocab"),
        P(None, "vocab"),
        P(DP, None),
        P(DP),
        P(DP),
    )
    out_specs = (P(DP, "vocab"), P(DP, None), P(None, DP, "vocab"), P(DP, "vocab"))
    return jax.shard_map(
        shards, mesh=finer, in_specs=in_specs, out_specs=out_specs, check_vma=False
    )
```

profile of v0, /device:TPU:1, one launch (start us, length us, event | category | flops | bytes accessed | tf_op | source)
XLA Modules:
  0.0 428.1 jit_solution(351393758666397825)
XLA Ops:
  7.2 0.0 copy-start
  7.2 0.0 all-gather.2.cloned.1.call-start
  7.2 1.5 copy-done
  8.8 2.1 fusion.3
  10.9 0.0 all-gather.2.cloned.1.call-update
  10.9 0.7 broadcast_subtract_fusion
  11.6 0.1 broadcast_in_dim.8
  11.7 0.1 sub.51
  11.8 52.5 %all-gather.2.cloned.1.call-done = bf16[128,4,2048]{2,0,1:T(8,128)(2,1)} async-done(((bf16[128,4,128]{2,0,1:T(8,128)(2,1)}), bf16[128,4,2048]{2,0,1:T(8,128)(2,1)}) %all-gather.2.cloned.1.call-update) | async-done | bytes 2097168 | tf_op jit(solution)/shard_map/all_gather | solution.py:52
  64.3 4.5 %copy.17 = bf16[128,4,2048]{2,1,0:T(4,128)(2,1)} copy(bf16[128,4,2048]{2,0,1:T(8,128)(2,1)} %all-gather.2.cloned.1.call-done) | data formatting | bytes 4194304 | tf_op jit(solution)/shard_map/all_gather | solution.py:52
  68.8 4.0 reshape.48
  72.8 15.1 %select_reduce_fusion = (f32[512]{0:T(512)S(1)}, f32[512,4096]{1,0:T(8,128)}) fusion(s32[512]{0:T(512)S(1)} %sub.51, bf16[512,2048]{1,0:T(8,128)(2,1)} %reshape.48, bf16[2048,4096]{1,0:T(8,128)(2,1)} %param.10), kind=kOutput, calls=%fused_computation.2 | convolution fusion | flops 8596226048 | bytes 27267072 | tf_op jit(solution)/shard_map/dot_general | solution.py:54
  87.9 0.1 reshape.49
  88.0 0.1 copy.18
  88.1 0.6 broadcast_in_dim.10
  88.7 3.9 all-to-all-start
  92.6 0.0 reduce-scatter.6.cloned.1.call-start
  92.7 0.0 copy-done.1
  92.7 0.0 copy-done.7
  92.7 0.3 exponential_reduce_fusion
  92.9 0.0 copy-start.3
  93.0 0.0 copy-done.10
  93.0 0.0 copy-start.11
  93.0 0.1 copy.20
  93.1 0.1 sub.53
  93.2 6.7 %all-to-all-done = f32[16,128,4]{1,2,0:T(4,128)S(1)} async-done(((f32[16,128,4]{1,2,0:T(4,128)}), f32[16,128,4]{1,2,0:T(4,128)S(1)}, u32[]{:S(2)}, u32[]{:S(2)}) %all-to-all-start) | async-done | bytes 32800 | tf_op jit(solution)/shard_map/all_to_all | solution.py:12
  100.0 0.0 copy-start.8
  100.0 0.0 copy-done.15
  100.0 0.1 copy.19
  100.1 0.1 mul.41
  100.2 16.1 %convolution_convert_fusion = bf16[2048,4096]{1,0:T(8,128)(2,1)} fusion(bf16[512,2048]{1,0:T(8,128)(2,1)} %reshape.48, f32[512,4096]{1,0:T(8,128)} %get-tuple-element.11, f32[512]{0:T(512)S(1)} %sub.53, f32[512]{0:T(512)S(1)} %mul.41, s32[512]{0:T(512)S(1)} %sub.51), kind=kOutput, calls=%fused_computation | convolution fusion | flops 8610906112 | bytes 27269120 | tf_op jit(solution)/shard_map/dot_general | solution.py:80
  116.3 0.0 reduce-scatter.6.cloned.1.call-update
  116.3 0.2 reduce-scatter.10.cloned.1.call-start
  116.5 16.7 %fusion = bf16[2048,512]{0,1:T(8,128)(2,1)} fusion(bf16[2048,4096]{1,0:T(8,128)(2,1)} %param.10, f32[512,4096]{1,0:T(8,128)} %get-tuple-element.11, f32[512]{0:T(512)S(1)} %sub.53, f32[512]{0:T(512)S(1)} %mul.41, s32[512]{0:T(512)S(1)} %sub.51), kind=kOutput, calls=%fused_computation.6 | convolution fusion | flops 8603566080 | bytes 27269120 | tf_op jit(solution)/shard_map/dot_general | solution.py:71
  133.3 4.0 copy.29
  137.2 0.0 reduce-scatter.10.cloned.1.call-update
  137.3 0.0 reduce-scatter.8.cloned.1.call-start
  137.3 124.4 %reduce-scatter.6.cloned.1.call-done = bf16[512,4096]{1,0:T(8,128)(2,1)} async-done(((bf16[2048,4096]{1,0:T(8,128)(2,1)}), bf16[512,4096]{1,0:T(8,128)(2,1)}) %reduce-scatter.6.cloned.1.call-update) | async-done | bytes 4194320 | tf_op jit(solution)/shard_map/reduce_scatter | solution.py:23
  261.7 0.0 reduce-scatter.8.cloned.1.call-update
  261.8 0.9 convolution_convert_fusion.3
  262.7 3.4 all-to-all-start.2
  266.2 68.4 %reduce-scatter.10.cloned.1.call-done = bf16[128,512]{1,0:T(8,128)(2,1)} async-done(((bf16[2048,512]{1,0:T(8,128)(2,1)}), bf16[128,512]{1,0:T(8,128)(2,1)}) %reduce-scatter.10.cloned.1.call-update) | async-done | bytes 131088
  334.6 0.0 copy-done.13
  334.6 1.0 copy.30
  335.6 0.8 fusion.2
  336.4 0.9 copy.42
  337.4 0.0 all-to-all-done.2
  337.4 7.2 %all-to-all-start.1 = ((bf16[16,128,128]{2,1,0:T(8,128)(2,1)}), bf16[16,128,128]{2,1,0:T(8,128)(2,1)S(1)}, u32[]{:S(2)}, u32[]{:S(2)}) async-start(bf16[16,128,128]{2,1,0:T(8,128)(2,1)} %bitcast.49), calls=%async_computation.1 | async-start | bytes 1048576 | tf_op jit(solution)/shard_map/all_to_all | solution.py:35
  344.5 0.7 convolution_convert_fusion.1
  345.3 0.0 copy-start.4
  345.3 0.0 copy-start.6
  345.3 0.0 copy-start.9
  345.3 0.0 copy-start.12
  345.3 0.0 copy-start.14
  345.3 1.6 copy.41
  346.9 8.6 %all-to-all-done.1 = bf16[16,128,128]{2,1,0:T(8,128)(2,1)S(1)} async-done(((bf16[16,128,128]{2,1,0:T(8,128)(2,1)}), bf16[16,128,128]{2,1,0:T(8,128)(2,1)S(1)}, u32[]{:S(2)}, u32[]{:S(2)}) %all-to-all-start.1) | async-done | bytes 524320 | tf_op jit(solution)/shard_map/all_to_all | solution.py:35
  355.5 4.3 %all-to-all-start.3 = ((bf16[8,4,256,128]{2,3,1,0:T(8,128)(2,1)}), bf16[8,4,256,128]{2,3,1,0:T(8,128)(2,1)}, u32[]{:S(2)}, u32[]{:S(2)}) async-start(bf16[8,4,256,128]{2,3,1,0:T(8,128)(2,1)} %bitcast.45), calls=%async_computation.3 | async-start | bytes 4194304 | tf_op jit(solution)/shard_map/all_to_all | solution.py:35
  359.9 0.6 convert_reduce_fusion.1
  360.5 0.1 convert_reduce_fusion
  360.6 1.6 fusion.4
  362.2 28.1 %all-to-all-done.3 = bf16[8,4,256,128]{2,3,1,0:T(8,128)(2,1)} async-done(((bf16[8,4,256,128]{2,3,1,0:T(8,128)(2,1)}), bf16[8,4,256,128]{2,3,1,0:T(8,128)(2,1)}, u32[]{:S(2)}, u32[]{:S(2)}) %all-to-all-start.3) | async-done | bytes 2097184 | tf_op jit(solution)/shard_map/all_to_all | solution.py:35
  390.4 1.9 reduce_sum.72
  392.3 0.8 copy.27
  393.1 28.4 %reduce-scatter.8.cloned.1.call-done = bf16[256,4096]{1,0:T(8,128)(2,1)} async-done(((bf16[512,4096]{1,0:T(8,128)(2,1)}), bf16[256,4096]{1,0:T(8,128)(2,1)}) %reduce-scatter.8.cloned.1.call-update) | async-done | bytes 2097168 | tf_op jit(solution)/shard_map/reduce_scatter | solution.py:23
  (23 shorter events, 0.1 us)
Async XLA Ops:
  7.2 1.6 copy-start
  7.2 57.1 %all-gather.2.cloned.1.call-start = ((), (), s32[]{:S(2)}) async-start(), calls=%async_computation.7 | async-start | bytes 2228224 | tf_op jit(solution)/shard_map/all_gather | solution.py:52
  72.8 19.9 %copy-start.1 = (bf16[128,2048]{1,0:T(8,128)(2,1)S(1)}, bf16[128,2048]{1,0:T(8,128)(2,1)}, u32[]{:S(2)}) copy-start(bf16[128,2048]{1,0:T(8,128)(2,1)} %param.7) | copy-start | bytes 1572868
  72.8 19.9 %copy-start.7 = (bf16[2048,4]{0,1:T(4,128)(2,1)S(1)}, bf16[2048,4]{0,1:T(4,128)(2,1)}, u32[]{:S(2)}) copy-start(bf16[2048,4]{0,1:T(4,128)(2,1)} %param.8) | copy-start | bytes 49156
  72.8 20.2 %copy-start.10 = (f32[128,4]{0,1:T(4,128)S(1)}, f32[128,4]{0,1:T(4,128)}, u32[]{:S(2)}) copy-start(f32[128,4]{0,1:T(4,128)} %param.11) | copy-start | bytes 6148
  72.8 27.2 %copy-start.15 = (f32[128]{0:T(128)S(1)}, f32[128]{0:T(128)}, u32[]{:S(2)}) copy-start(f32[128]{0:T(128)} %param.13) | copy-start | bytes 1540
  88.7 11.2 %all-to-all-start = ((f32[16,128,4]{1,2,0:T(4,128)}), f32[16,128,4]{1,2,0:T(4,128)S(1)}, u32[]{:S(2)}, u32[]{:S(2)}) async-start(f32[16,128,4]{1,2,0:T(4,128)} %broadcast_in_dim.10), calls=%async_computation | async-start | bytes 65536 | tf_op jit(solution)/shard_map/all_to_all | solution.py:12
  92.6 169.1 %reduce-scatter.6.cloned.1.call-start = ((), (), s32[]{:S(2)}) async-start(), calls=%async_computation.8 | async-start | bytes 20971520 | tf_op jit(solution)/shard_map/reduce_scatter | solution.py:23
  92.9 168.8 %copy-start.3 = (f32[128,4]{0,1:T(4,128)}, f32[128,4]{0,1:T(4,128)S(1)}, u32[]{:S(2)}) copy-start(f32[128,4]{0,1:T(4,128)S(1)} %get-tuple-element.13) | copy-start | bytes 6148
  93.0 168.8 %copy-start.11 = (f32[128]{0:T(128)}, f32[128]{0:T(128)S(1)}, u32[]{:S(2)}) copy-start(f32[128]{0:T(128)S(1)} %log.8) | copy-start | bytes 1540
  100.0 161.8 %copy-start.5 = (f32[128,4]{0,1:T(4,128)}, f32[128,4]{0,1:T(4,128)S(1)}, u32[]{:S(2)}) copy-start(f32[128,4]{0,1:T(4,128)S(1)} %get-tuple-element.9) | copy-start | bytes 6148
  100.0 161.8 %copy-start.8 = (f32[128]{0:T(128)}, f32[128]{0:T(128)S(1)}, u32[]{:S(2)}) copy-start(f32[128]{0:T(128)S(1)} %get-tuple-element.8) | copy-start | bytes 1540
  116.3 218.2 %reduce-scatter.10.cloned.1.call-start = ((), (), s32[]{:S(2)}) async-start(), calls=%async_computation.10 | async-start | bytes 2228224
  133.3 202.3 %copy-start.2 = (bf16[128,4,128]{2,0,1:T(8,128)(2,1)S(1)}, bf16[128,4,128]{2,0,1:T(8,128)(2,1)}, u32[]{:S(2)}) copy-start(bf16[128,4,128]{2,0,1:T(8,128)(2,1)} %fusion.3) | copy-start | bytes 393220
  137.3 284.3 %reduce-scatter.8.cloned.1.call-start = ((), (), s32[]{:S(2)}) async-start(), calls=%async_computation.9 | async-start | bytes 6291456 | tf_op jit(solution)/shard_map/reduce_scatter | solution.py:23
  261.8 72.8 %copy-start.13 = (f32[128]{0:T(128)}, f32[128]{0:T(128)S(1)}, u32[]{:S(2)}) copy-start(f32[128]{0:T(128)S(1)} %neg.4) | copy-start | bytes 1540
  262.7 74.7 %all-to-all-start.2 = ((bf16[8,256,4]{1,2,0:T(4,128)(2,1)}), bf16[8,256,4]{1,2,0:T(4,128)(2,1)S(1)}, u32[]{:S(2)}, u32[]{:S(2)}) async-start(bf16[8,256,4]{1,2,0:T(4,128)(2,1)} %bitcast.7), calls=%async_computation.2 | async-start | bytes 32768 | tf_op jit(solution)/shard_map/all_to_all | solution.py:35
  337.4 18.2 %all-to-all-start.1 = ((bf16[16,128,128]{2,1,0:T(8,128)(2,1)}), bf16[16,128,128]{2,1,0:T(8,128)(2,1)S(1)}, u32[]{:S(2)}, u32[]{:S(2)}) async-start(bf16[16,128,128]{2,1,0:T(8,128)(2,1)} %bitcast.49), calls=%async_computation.1 | async-start | bytes 1048576 | tf_op jit(solution)/shard_map/all_to_all | solution.py:35
  345.3 15.3 %copy-start.4 = (f32[128,4]{0,1:T(4,128)S(1)}, f32[128,4]{0,1:T(4,128)}, u32[]{:S(2)}) copy-start(f32[128,4]{0,1:T(4,128)} %copy-done.3) | copy-start | bytes 6148
  345.3 15.3 %copy-start.6 = (f32[128,4]{0,1:T(4,128)S(1)}, f32[128,4]{0,1:T(4,128)}, u32[]{:S(2)}) copy-start(f32[128,4]{0,1:T(4,128)} %copy-done.5) | copy-start | bytes 6148
  345.3 15.3 %copy-start.9 = (f32[128]{0:T(128)S(1)}, f32[128]{0:T(128)}, u32[]{:S(2)}) copy-start(f32[128]{0:T(128)} %copy-done.8) | copy-start | bytes 1540
  345.3 15.3 %copy-start.12 = (f32[128]{0:T(128)S(1)}, f32[128]{0:T(128)}, u32[]{:S(2)}) copy-start(f32[128]{0:T(128)} %copy-done.11) | copy-start | bytes 1540
  345.3 15.3 %copy-start.14 = (f32[128]{0:T(128)S(1)}, f32[128]{0:T(128)}, u32[]{:S(2)}) copy-start(f32[128]{0:T(128)} %copy-done.13) | copy-start | bytes 1540
  355.5 34.8 %all-to-all-start.3 = ((bf16[8,4,256,128]{2,3,1,0:T(8,128)(2,1)}), bf16[8,4,256,128]{2,3,1,0:T(8,128)(2,1)}, u32[]{:S(2)}, u32[]{:S(2)}) async-start(bf16[8,4,256,128]{2,3,1,0:T(8,128)(2,1)} %bitcast.45), calls=%async_computation.3 | async-start | bytes 4194304 | tf_op jit(solution)/shard_map/all_to_all | solution.py:35
Sparse Core Ops, SparseCore 0:
  11.1 53.1 all-gather.1
  116.4 145.2 reduce-scatter.5
  265.7 68.8 reduce-scatter.9
  337.4 84.1 reduce-scatter.7
where the time goes:
time: 429 us; the launch traced here: 428 us
  waiting for transfers between devices  317 us (74%)
  matrix products  54.3 us (13%)
  local copies, waits for them, and re-layouts  19.9 us (5%)
  starting transfers between devices  19.2 us (4%)
  between operations  14.1 us (3%)
    reduce_scatter x2, waiting for transfers between devices, sum_by_axis(): subtotal = lax.psum_scatter(subtotal, axis, scatter_dimension=0, tiled=True)  153 us
    unnamed x5, waiting for transfers between devices  68.4 us
    all_gather x1, waiting for transfers between devices, shards(): comp_all = lax.all_gather(comp_local, 'vocab', axis=2, tiled=True)  52.5 us
    all_to_all x3, waiting for transfers between devices, sum_at_owner(): parts = lax.all_to_all(in_blocks(array, dim, count), axis, 0, 0, tiled=True)  36.8 us
    dot_general x1, matrix products, shards(): lax.dot_general(part_rows, grad_logits, (((1,), (1,)), ((), ())), preferr...  16.7 us
    dot_general x1, matrix products, shards(): lax.dot_general(part_rows, grad_logits, (((0,), (0,)), ((), ())), preferr...  16.1 us
    dot_general x1, matrix products, shards(): logits = jnp.dot(comp_rows, out_weight, preferred_element_type=jnp.float32)  15.1 us
    all_to_all x3, starting transfers between devices, sum_at_owner(): parts = lax.all_to_all(in_blocks(array, dim, count), axis, 0, 0, tiled=True)  15 us
  transfers between devices with their start and end apart: 8, of which 7 were waited for; matrix products, arithmetic and copies ran while one was open for 8% of the time, Pallas kernels for 0%

commit v1 on v0

v1 whole, which is shorter than its diff:
```python
import functools

import jax
import jax.numpy as jnp
from jax import lax
from jax.experimental import pallas as pl
from jax.experimental.pallas import tpu as pltpu
from jax.sharding import Mesh
from jax.sharding import PartitionSpec as P

AXES = ("x", "zl", "zh", "y", "c")
DP = ("x", "zl")
VOC = ("zh", "y", "c")
MESH_ID = pl.DeviceIdType.MESH
F32 = jnp.float32
BF16 = jnp.bfloat16

T = 128
K = 4
R = T * K
U = 128
D = 2048
VL = 4096
VH = VL // 2
NC = 8
C = VH // NC


def nt(a, b):
    return lax.dot_general(a, b, (((1,), (1,)), ((), ())), preferred_element_type=F32)


def nn(a, b):
    return lax.dot_general(a, b, (((1,), (0,)), ((), ())), preferred_element_type=F32)


def kernel(
    mix_t,
    lse_t,
    scale,
    target,
    hidden_hbm,
    proj_hbm,
    w_hbm,
    gh_out,
    gm_out,
    gp_out,
    go_out,
    hidden,
    proj,
    w,
    comp,
    comp_t,
    gl,
    part,
    r1x,
    rfx,
    gcb,
    rd,
    r1a,
    rfa,
    r1b,
    rfb,
    wt,
    hs,
    hst,
    gpx,
    gpall,
    prods,
    prodr,
    gms,
    gmr,
    hts,
    hrecv,
    info2,
    lsec,
    coefc,
    tgtc,
    tl,
    pbuf,
    gh_v,
    gm_v,
    gp_v,
    sem_w,
    sem_i,
    p_s,
    p_r,
    sem_o,
    ag_s,
    ag_r,
    hs_s,
    hs_r,
    tl_s,
    tl_r,
    x_s,
    x_r,
    zx_s,
    zx_r,
    zx_l,
    d_s,
    d_r,
    a_s,
    a_r,
    b_s,
    b_r,
    h_s,
    h_r,
    g_s,
    g_r,
):
    x = lax.axis_index("x")
    zl = lax.axis_index("zl")
    zh = lax.axis_index("zh")
    y = lax.axis_index("y")
    c = lax.axis_index("c")
    z = zh * 2 + zl
    v = zh * 8 + y * 2 + c
    d = x * 2 + zl

    def m4(i):
        return lax.rem(i + 4, 4)

    def dev(x_=None, z_=None, y_=None, c_=None):
        zz = z if z_ is None else z_
        return (
            x if x_ is None else x_,
            lax.rem(zz, 2),
            lax.div(zz, 2),
            y if y_ is None else y_,
            c if c_ is None else c_,
        )

    def rc(src, dst, ss, rs, to):
        return pltpu.make_async_remote_copy(
            src_ref=src, dst_ref=dst, send_sem=ss, recv_sem=rs, device_id=to, device_id_type=MESH_ID
        )

    partner_c = dev(c_=1 - c)
    partner_z = (x, 1 - zl, zh, y, c)

    q32 = z * 8 + y * 2 + c

    def mate(o):
        p = lax.rem(q32 + o, 32)
        zz = lax.div(p, 8)
        return (x, lax.rem(zz, 2), lax.div(zz, 2), lax.rem(lax.div(p, 2), 4), lax.rem(p, 2))

    barrier = pltpu.get_barrier_semaphore()

    def greet(o, carry):
        pl.semaphore_signal(barrier, inc=1, device_id=mate(o), device_id_type=MESH_ID)
        return carry

    lax.fori_loop(1, 32, greet, 0)
    for o in range(1, 4):
        pl.semaphore_signal(barrier, inc=1, device_id=dev(x_=m4(x + o)), device_id_type=MESH_ID)

    hidden_copy = pltpu.make_async_copy(hidden_hbm, hidden, sem_w.at[0])
    proj_copy = pltpu.make_async_copy(proj_hbm, proj, sem_w.at[1])
    w_copy = pltpu.make_async_copy(
        w_hbm.at[:, pl.ds(pl.multiple_of(zl * VH, VH), VH)], w, sem_w.at[2]
    )
    hidden_copy.start()
    proj_copy.start()
    w_copy.start()
    hidden_copy.wait()
    mix_logits = nt(mix_t[...], hidden[...])
    info2[zl, 0:4] = lse_t[...]
    info2[zl, 4:8] = mix_logits - jnp.log(jnp.sum(jnp.exp(mix_logits), axis=0, keepdims=True))
    info2[zl, 8:9] = scale[...]
    info2[zl, 9:10] = target[...].astype(F32)
    info2[zl, 10:16] = jnp.zeros((6, T), F32)

    def row_columns(g):
        cols = jnp.transpose(jnp.concatenate([info2[g], jnp.zeros((112, T), F32)], axis=0))
        local = cols[:, 9:10] - (v * VL + zl * VH).astype(F32)
        for k in range(K):
            rows = pl.ds(pl.multiple_of(g * R + k * T, T), T)
            lsec[rows, :] = jnp.broadcast_to(cols[:, k : k + 1], (T, 128))
            tgtc[rows, :] = jnp.broadcast_to(local, (T, 128))

    row_columns(zl)
    info_copy = rc(info2.at[zl], info2.at[zl], sem_i.at[0], sem_i.at[1], partner_z)

    own_rows = pl.multiple_of(zl * R, R)
    own_cols = pl.multiple_of(v * U, U)

    def blk(col, z_, y_, c_, r0=0, n=2 * T):
        row = lax.rem(z_, 2) * R + col * 2 * T + r0
        lane = (lax.div(z_, 2) * 8 + y_ * 2 + c_) * U
        return comp.at[pl.ds(pl.multiple_of(row, T), n), pl.ds(pl.multiple_of(lane, U), U)]

    def pos(col):
        return (y, z) if col == 0 else (z, y)

    def at_ab(col, a_, b_, c_, r0=0, n=2 * T):
        return blk(col, b_, a_, c_, r0, n) if col == 0 else blk(col, a_, b_, c_, r0, n)

    def dev_ab(col, a_, b_):
        return dev(y_=a_, z_=b_) if col == 0 else dev(z_=a_, y_=b_)

    def ag_copy(col, i, ref, to):
        return rc(ref, ref, ag_s.at[col * 36 + i], ag_r.at[col * 36 + i], to)

    ag_sent = []

    def ag_send(col, i, ref, to):
        cp = ag_copy(col, i, ref, to)
        cp.start()
        ag_sent.append(cp)

    def ag_wait(col, i, ref):
        ag_copy(col, i, ref, partner_c).wait_recv()

    def second(col, i, ref):
        a, b = pos(col)
        ag_send(col, 4 + 4 * i, ref, dev_ab(col, a, m4(b + 1)))
        ag_send(col, 4 + 4 * i + 1, ref, dev_ab(col, a, m4(b - 1)))

    def across(col, i, j, ref):
        ag_send(col, 20 + i * 4 + j, ref, partner_c)

    proj_copy.wait()
    for k in range(K):
        pre = nn(hidden[...], proj[k])
        comp[pl.ds(pl.multiple_of(own_rows + k * T, T), T), pl.ds(own_cols, U)] = jnp.tanh(
            pre
        ).astype(BF16)
    pl.semaphore_wait(barrier, 34)
    for col in range(2):
        a, b = pos(col)
        own = at_ab(col, a, b, c)
        ag_send(col, 0, own, dev_ab(col, m4(a + 1), b))
        ag_send(col, 1, own, dev_ab(col, m4(a - 1), b))
    info_copy.start()
    for col in range(2):
        a, b = pos(col)
        own = at_ab(col, a, b, c)
        second(col, 0, own)
        across(col, 0, 0, own)

    def hs_copy(i):
        p = m4(x + (0, 1, -1, 2)[i])
        return rc(
            hidden.at[:, pl.ds(pl.multiple_of(p * 512, 512), 512)],
            hs.at[i],
            hs_s.at[i],
            hs_r.at[i],
            dev(x_=p),
        )

    for i in range(1, 4):
        hs_copy(i).start()
    hs[0] = hidden[:, pl.ds(pl.multiple_of(x * 512, 512), 512)]

    def pick(n, carry):
        rows = pl.ds(pl.multiple_of(n * 512, 512), 512)
        acc = jnp.zeros((2 * T, 512), F32)
        for q in range(4):
            lane = lax.broadcasted_iota(jnp.int32, (T, 512), 1).astype(F32) + float(q * 512)
            hot = jnp.concatenate(
                [
                    (lane == tgtc[pl.ds(g * R, T), :][:, 0:1]).astype(F32).astype(BF16)
                    for g in range(2)
                ],
                axis=0,
            )
            acc = acc + nt(hot, w[rows, pl.ds(q * 512, 512)])
        wt[:, rows] = acc.astype(BF16)
        return carry

    for col in range(2):
        a, b = pos(col)
        prev, nxt = m4(a - 1), m4(a + 1)
        ag_wait(col, 0, at_ab(col, prev, b, c))
        ag_send(col, 2, at_ab(col, prev, b, c, 0, T), dev_ab(col, nxt, b))
        second(col, 1, at_ab(col, prev, b, c))
        across(col, 1, 0, at_ab(col, prev, b, c))
        ag_wait(col, 1, at_ab(col, nxt, b, c))
        ag_send(col, 3, at_ab(col, nxt, b, c, T, T), dev_ab(col, prev, b))
        second(col, 2, at_ab(col, nxt, b, c))
        across(col, 2, 0, at_ab(col, nxt, b, c))
    info_in = rc(info2.at[1 - zl], info2.at[1 - zl], sem_i.at[0], sem_i.at[1], partner_z)
    info_in.wait_recv()
    row_columns(1 - zl)
    w_copy.wait()
    lax.fori_loop(0, 4, pick, 0)
    for col in range(2):
        a, b = pos(col)
        far = m4(a + 2)
        ag_wait(col, 2, at_ab(col, far, b, c, 0, T))
        ag_wait(col, 3, at_ab(col, far, b, c, T, T))
        second(col, 3, at_ab(col, far, b, c))
        across(col, 3, 0, at_ab(col, far, b, c))
    for i in range(4):
        for col in range(2):
            a, b = pos(col)
            a_ = m4(a + (0, -1, 1, 2)[i])
            prev, nxt = m4(b - 1), m4(b + 1)
            ag_wait(col, 4 + 4 * i, at_ab(col, a_, prev, c))
            ag_send(col, 4 + 4 * i + 2, at_ab(col, a_, prev, c, 0, T), dev_ab(col, a, nxt))
            across(col, i, 1, at_ab(col, a_, prev, c))
            ag_wait(col, 4 + 4 * i + 1, at_ab(col, a_, nxt, c))
            ag_send(col, 4 + 4 * i + 3, at_ab(col, a_, nxt, c, T, T), dev_ab(col, a, prev))
            across(col, i, 2, at_ab(col, a_, nxt, c))
    for i in range(4):
        for col in range(2):
            a, b = pos(col)
            a_ = m4(a + (0, -1, 1, 2)[i])
            far = m4(b + 2)
            ag_wait(col, 4 + 4 * i + 2, at_ab(col, a_, far, c, 0, T))
            ag_wait(col, 4 + 4 * i + 3, at_ab(col, a_, far, c, T, T))
            across(col, i, 3, at_ab(col, a_, far, c))
    for i in range(4):
        for j in range(4):
            for col in range(2):
                a, b = pos(col)
                a_ = m4(a + (0, -1, 1, 2)[i])
                b_ = m4(b + (0, -1, 1, 2)[j])
                ag_wait(col, 20 + i * 4 + j, at_ab(col, a_, b_, 1 - c))

    lane_t = lax.broadcasted_iota(jnp.int32, (T, 128), 1)
    acc = jnp.zeros((T, 128), F32)
    for g in range(2):
        for k in range(K):
            s = jnp.zeros((T, 128), F32)
            for q in range(4):
                prod = comp[pl.ds(g * R + k * T, T), pl.ds(q * 512, 512)].astype(F32) * wt[
                    pl.ds(g * T, T), pl.ds(q * 512, 512)
                ].astype(F32)
                for e in range(4):
                    s = s + prod[:, e * 128 : (e + 1) * 128]
            acc = jnp.where(lane_t == g * K + k, jnp.sum(s, axis=1, keepdims=True), acc)
    tl[0] = jnp.transpose(acc)[0:8]

    def tl_copy(o):
        return rc(tl.at[0], tl.at[o], tl_s.at[o], tl_r.at[o], mate(o))

    def tl_start(o, carry):
        tl_copy(o).start()
        return carry

    lax.fori_loop(1, 32, tl_start, 0)

    def flip(n, carry):
        cols = pl.ds(pl.multiple_of(n * U, U), U)
        for m in range(2):
            comp_t[cols, pl.ds(m * R, R)] = jnp.transpose(comp[pl.ds(m * R, R), cols])
        return carry

    lax.fori_loop(0, D // U, flip, 0)

    lane_w = lax.broadcasted_iota(jnp.int32, (2 * T, 128), 1).astype(F32)

    def chunk_logits(cc, m, put):
        rows = pl.ds(pl.multiple_of(m * 2 * T, 2 * T), 2 * T)
        logit = nn(comp[rows, :], w[:, pl.ds(pl.multiple_of(cc * C, C), C)])
        shift = jnp.asarray(cc * C, F32)
        lse_m, tgt_m = lsec[rows, :], tgtc[rows, :] - shift
        for e in range(C // 128):
            prob = jnp.exp(logit[:, e * 128 : (e + 1) * 128] - lse_m)
            hot = jnp.where(lane_w + float(e * 128) == tgt_m, 1.0, 0.0)
            put(rows, e, prob - hot)

    def hold(m, carry):
        def put(rows, e, val):
            pbuf[rows, pl.ds(e * 128, 128)] = val

        chunk_logits(0, m, put)
        return carry

    lax.fori_loop(0, 4, hold, 0)

    def tl_wait(o, carry):
        tl_copy(o).wait()
        return carry

    lax.fori_loop(1, 32, tl_wait, 0)
    target_logit = jnp.sum(tl[...], axis=0)
    coef_rows = []
    gml_rows = []
    for g in range(2):
        lse_g = info2[g, 0:4]
        lm_g = info2[g, 4:8]
        scale_g = info2[g, 8:9]
        weights = jnp.exp(lm_g + target_logit[g * K : (g + 1) * K] - lse_g)
        resp = weights / jnp.sum(weights, axis=0, keepdims=True)
        coef_rows.append(scale_g * resp)
        gml_rows.append(-scale_g * (resp - jnp.exp(lm_g)))
    table = jnp.concatenate(coef_rows + gml_rows + [jnp.zeros((112, 128), F32)], axis=0)
    cols = jnp.transpose(table)
    for g in range(2):
        for k in range(K):
            coefc[pl.ds(g * R + k * T, T), :] = jnp.broadcast_to(
                cols[:, g * K + k : g * K + k + 1], (T, 128)
            )
    gml = jnp.zeros((T, 128), F32)
    for k in range(K):
        mine = jnp.where(zl == 0, cols[:, 8 + k : 9 + k], cols[:, 12 + k : 13 + k])
        high = mine.astype(BF16).astype(F32)
        gml = jnp.where(lane_t == k, high, gml)
        gml = jnp.where(lane_t == K + k, mine - high, gml)
    gpx[4] = gml.astype(BF16)

    def ring(idx, n, piece, me, right, left, r1, rf, ss, rs):
        two, one, back = m4(me + 2), m4(me + 1), m4(me - 1)
        copies = (
            lambda: rc(piece(two, 0), r1(0), ss.at[idx], rs.at[idx], right),
            lambda: rc(piece(one, 1), rf(0, 1), ss.at[idx + 1], rs.at[idx + 1], right),
            lambda: rc(piece(two, 1), r1(1), ss.at[idx + 2], rs.at[idx + 2], left),
            lambda: rc(piece(back, 0), rf(1, 0), ss.at[idx + 3], rs.at[idx + 3], left),
            lambda: rc(piece(one, 0), rf(0, 0), ss.at[idx + 4], rs.at[idx + 4], right),
            lambda: rc(piece(back, 1), rf(1, 1), ss.at[idx + 5], rs.at[idx + 5], left),
        )

        def first(which=(0, 2, 1, 3)):
            for i in which:
                copies[i]().start()

        def add(ref, other):
            ref[...] = (ref[...].astype(F32) + other[...].astype(F32)).astype(BF16)

        def forward():
            copies[0]().wait_recv()
            add(piece(one, 0), r1(0))
            copies[4]().start()
            copies[2]().wait_recv()
            add(piece(back, 1), r1(1))
            copies[5]().start()

        def arrive():
            for i in (1, 3, 4, 5):
                copies[i]().wait_recv()

        def drain():
            for i in range(6):
                copies[i]().wait_send()

        return first, forward, arrive, drain

    x_right, x_left = dev(x_=m4(x + 1)), dev(x_=m4(x - 1))

    def x_ring(cc):
        return ring(
            cc * 6,
            6,
            lambda t, h: part.at[cc, t * 2 + h],
            x,
            x_right,
            x_left,
            lambda i: r1x.at[cc, i],
            lambda i, h: rfx.at[cc, i, h],
            x_s,
            x_r,
        )

    def chunk_out(cc):
        cols = pl.ds(pl.multiple_of(cc * C, C), C)
        for i in range(4):
            t = m4(x + (2, 1, -1, 0)[i])
            rows = pl.ds(pl.multiple_of(t * 512, 512), 512)
            res = nn(comp_t[rows, :], gl[:, cols]).astype(BF16)
            part[cc, t * 2] = res[0:256]
            part[cc, t * 2 + 1] = res[256:512]
            if i < 3:
                x_ring(cc)[0](((0, 2), (1,), (3,))[i])

    def scale_first(m, carry):
        rows = pl.ds(pl.multiple_of(m * 2 * T, 2 * T), 2 * T)
        coef_m = coefc[rows, :]
        for e in range(C // 128):
            gl[rows, pl.ds(e * 128, 128)] = (coef_m * pbuf[rows, pl.ds(e * 128, 128)]).astype(BF16)
        return carry

    lax.fori_loop(0, 4, scale_first, 0)
    chunk_out(0)

    def chunk(cc, carry):
        def rows_of(m, carry2):
            coef_m = coefc[pl.ds(pl.multiple_of(m * 2 * T, 2 * T), 2 * T), :]

            def put(rows, e, val):
                gl[rows, pl.ds(pl.multiple_of(cc * C + e * 128, 128), 128)] = (coef_m * val).astype(
                    BF16
                )

            chunk_logits(cc, m, put)
            return carry2

        lax.fori_loop(0, 4, rows_of, 0)
        chunk_out(cc)
        return carry

    lax.fori_loop(1, NC, chunk, 0)

    def comp_grad(col):
        def tile(i, carry):
            g, h, j = lax.div(i, 4), lax.rem(lax.div(i, 2), 2), lax.rem(i, 2)
            rows = pl.ds(pl.multiple_of(g * R + col * 2 * T, 2 * T), 2 * T)
            units = pl.ds(pl.multiple_of((h * 2 + j) * 512, 512), 512)
            res = nt(gl[rows, :], w[units, :])
            z_ = h * 2 + g
            for jj in range(4):
                y_ = j * 2 + jj // 2
                val = res[:, jj * 128 : (jj + 1) * 128].astype(BF16)
                if col == 0:
                    gcb[jj % 2, col, z_, y_] = val
                else:
                    gcb[jj % 2, col, y_, z_] = val
            return carry

        lax.fori_loop(0, 8, tile, 0)
        swap = rc(gcb.at[1 - c, col], rd.at[col], d_s.at[col], d_r.at[col], partner_c)
        swap.start()
        return swap

    def a_ring(col):
        me = z if col == 0 else y
        mk = (lambda p: dev(z_=p)) if col == 0 else (lambda p: dev(y_=p))
        return ring(
            col * 6,
            6,
            lambda t, h: gcb.at[c, col, t, pl.ds(2 * h, 2)],
            me,
            mk(m4(me + 1)),
            mk(m4(me - 1)),
            lambda i: r1a.at[col, i],
            lambda i, h: rfa.at[col, i, h],
            a_s,
            a_r,
        )

    def b_ring(col):
        first = z if col == 0 else y
        me = y if col == 0 else z
        mk = (lambda p: dev(y_=p)) if col == 0 else (lambda p: dev(z_=p))
        return ring(
            col * 6,
            6,
            lambda t, h: gcb.at[c, col, first, t, pl.ds(h * T, T)],
            me,
            mk(m4(me + 1)),
            mk(m4(me - 1)),
            lambda i: r1b.at[col, i],
            lambda i, h: rfb.at[col, i, h],
            b_s,
            b_r,
        )

    def merge(col, swap):
        swap.wait_recv()

        def add(i, carry):
            p, q = lax.div(i, 4), lax.rem(i, 4)
            gcb[c, col, p, q] = (gcb[c, col, p, q].astype(F32) + rd[col, p, q].astype(F32)).astype(
                BF16
            )
            return carry

        lax.fori_loop(0, 16, add, 0)

    def finish_a(col):
        me = z if col == 0 else y
        for h in range(2):
            for e in range(2):
                q = 2 * h + e
                gcb[c, col, me, q] = (
                    gcb[c, col, me, q].astype(F32)
                    + rfa[col, 0, h, e].astype(F32)
                    + rfa[col, 1, h, e].astype(F32)
                ).astype(BF16)

    def x_finish(cc):
        x_ring(cc)[2]()
        for h in range(2):
            part[cc, x * 2 + h] = (
                part[cc, x * 2 + h].astype(F32)
                + rfx[cc, 0, h].astype(F32)
                + rfx[cc, 1, h].astype(F32)
            ).astype(BF16)
        for cp in z_copies(cc):
            cp.start()

    def z_copies(cc):
        cols = pl.ds(pl.multiple_of(zl * VH + cc * C, C), C)
        dst = go_out.at[:, cols]
        return (
            rc(part.at[cc, x * 2 + 1 - zl], dst, zx_s.at[cc], zx_r.at[cc], partner_z),
            pltpu.make_async_copy(part.at[cc, x * 2 + zl], dst, zx_l.at[cc]),
        )

    for cc in range(4):
        x_ring(cc)[1]()
    swap0 = comp_grad(0)
    x_ring(4)[1]()
    swap1 = comp_grad(1)
    x_ring(5)[1]()
    merge(0, swap0)
    a_ring(0)[0]()
    merge(1, swap1)
    a_ring(1)[0]()
    a_ring(0)[1]()
    a_ring(1)[1]()
    for i in range(1, 4):
        hs_copy(i).wait()
    for i in range(4):
        hst[:, pl.ds(i * T, T)] = jnp.transpose(hs[i])
    x_ring(6)[1]()
    a_ring(0)[2]()
    finish_a(0)
    b_ring(0)[0]()
    a_ring(1)[2]()
    finish_a(1)
    b_ring(1)[0]()
    b_ring(0)[1]()
    b_ring(1)[1]()
    x_finish(0)

    for col in range(2):
        first = z if col == 0 else y
        me = y if col == 0 else z
        b_ring(col)[2]()
        for h in range(2):
            total = (
                gcb[c, col, first, me, pl.ds(h * T, T)].astype(F32)
                + rfb[col, 0, h].astype(F32)
                + rfb[col, 1, h].astype(F32)
            )
            k = 2 * col + h
            cf = comp[
                pl.ds(pl.multiple_of(own_rows + k * T, T), T), pl.ds(own_cols, U)
            ].astype(F32)
            gpx[k] = (total * (1.0 - cf * cf)).astype(BF16)

    def slot(i, r0=0, n=T):
        return gpall.at[:, pl.ds(i * T + r0, n)]

    g_copies = (
        rc(gpx, slot(1), g_s.at[0], g_r.at[0], x_right),
        rc(gpx, slot(2), g_s.at[1], g_r.at[1], x_left),
        rc(slot(1, 0, T // 2), slot(3, 0, T // 2), g_s.at[2], g_r.at[2], x_right),
        rc(slot(2, T // 2, T // 2), slot(3, T // 2, T // 2), g_s.at[3], g_r.at[3], x_left),
    )
    g_copies[0].start()
    g_copies[1].start()
    x_ring(7)[1]()

    def h_copy(o):
        p = lax.rem(v + o, 16)
        to = (x, zl, lax.div(p, 8), lax.rem(lax.div(p, 2), 4), lax.rem(p, 2))
        return rc(hts.at[o], hrecv.at[o], h_s.at[o], h_r.at[o], to)

    def h_tile(o):
        p = lax.rem(v + o, 16)
        rows = pl.ds(pl.multiple_of(p * U, U), U)
        acc = nt(gpx[0], proj[0, rows, :])
        for k in range(1, K):
            acc = acc + nt(gpx[k], proj[k, rows, :])
        return acc

    def h_step(o, carry):
        hts[o] = h_tile(o).astype(BF16)
        h_copy(o).start()
        return carry

    lax.fori_loop(1, 16, h_step, 0)
    hrecv[0] = h_tile(0).astype(BF16)
    gpall[:, pl.ds(0, T)] = gpx[...]
    x_finish(1)
    x_finish(2)
    x_finish(3)
    g_copies[0].wait_recv()
    g_copies[2].start()
    g_copies[1].wait_recv()
    g_copies[3].start()

    def h_wait(o, carry):
        h_copy(o).wait()
        return carry

    lax.fori_loop(1, 16, h_wait, 0)
    mw = jnp.concatenate(
        [mix_t[:, pl.ds(own_cols, U)].astype(F32)] * 2 + [jnp.zeros((120, U), F32)], axis=0
    ).astype(BF16)
    gh = nn(gpx[4], mw)
    for o in range(16):
        gh = gh + hrecv[o].astype(F32)
    gh_v[...] = gh.astype(BF16)
    out_copies = (
        pltpu.make_async_copy(gh_v, gh_out, sem_o.at[0]),
        pltpu.make_async_copy(gp_v, gp_out, sem_o.at[1]),
        pltpu.make_async_copy(gm_v, gm_out, sem_o.at[2]),
    )
    out_copies[0].start()
    x_finish(4)
    x_finish(5)

    g_copies[2].wait_recv()
    g_copies[3].wait_recv()

    def product(half, k):
        return nn(hst[pl.ds(pl.multiple_of(half * 256, 256), 256), :], gpall[k])

    def mix_product(half):
        res = lax.dot_general(
            gpall[4],
            hst[pl.ds(pl.multiple_of(half * 256, 256), 256), :],
            (((0,), (1,)), ((), ())),
            preferred_element_type=F32,
        )
        return res[0:4] + res[4:8]

    for k in range(K):
        prods[k] = product(1 - zl, k).astype(BF16)
    gms[...] = mix_product(1 - zl)
    p_copies = (
        rc(prods, prodr, p_s.at[0], p_r.at[0], partner_z),
        rc(gms, gmr, p_s.at[1], p_r.at[1], partner_z),
    )
    for cp in p_copies:
        cp.start()
    x_finish(6)
    x_finish(7)
    for cp in p_copies:
        cp.wait_recv()
    for k in range(K):
        gp_v[k] = (product(zl, k) + prodr[k].astype(F32)).astype(BF16)
    gm_v[...] = mix_product(zl) + gmr[...]
    out_copies[1].start()
    out_copies[2].start()

    for cp in ag_sent:
        cp.wait_send()
    for cp in (info_copy, swap0, swap1, *g_copies, *p_copies):
        cp.wait_send()
    for col in range(2):
        a_ring(col)[3]()
        b_ring(col)[3]()

    def x_drain(cc, carry):
        x_ring(cc)[3]()
        for cp in z_copies(cc):
            cp.wait()
        return carry

    lax.fori_loop(0, NC, x_drain, 0)
    for cp in out_copies:
        cp.wait()


def place(gh, gm, gp, go, gh_o, gm_o, gp_o, go_o, b_gh, b_gm, b_gp, b_go, s_in, s_out):
    pairs = [(gh, b_gh, gh_o), (gm, b_gm, gm_o), (gp, b_gp, gp_o)]
    for i in range(4):
        rows = pl.ds(i * 64, 64)
        pairs.append((go.at[rows], b_go.at[rows], go_o.at[rows]))
    loads = [pltpu.make_async_copy(s, b, s_in.at[i]) for i, (s, b, _) in enumerate(pairs)]
    stores = [pltpu.make_async_copy(b, t, s_out.at[i]) for i, (_, b, t) in enumerate(pairs)]
    for cp in reversed(loads):
        cp.start()
    for i in reversed(range(len(pairs))):
        loads[i].wait()
        stores[i].start()
    for cp in stores:
        cp.wait()


def shards(hidden, mix_weight, proj_weight, out_weight, saved_lse, targets, loss_scale):
    vm = pl.BlockSpec(memory_space=pltpu.VMEM)
    hbm = pl.BlockSpec(memory_space=pltpu.HBM)
    dma = pltpu.SemaphoreType.DMA
    outs = (
        jax.ShapeDtypeStruct((T, U), BF16),
        jax.ShapeDtypeStruct((K, 256), F32),
        jax.ShapeDtypeStruct((K, 256, U), BF16),
        jax.ShapeDtypeStruct((256, VL), BF16),
    )
    found = pl.pallas_call(
        kernel,
        out_shape=outs,
        in_specs=[vm, vm, vm, vm, hbm, hbm, hbm],
        out_specs=(hbm, hbm, hbm, hbm),
        scratch_shapes=[
            pltpu.VMEM((T, D), BF16),
            pltpu.VMEM((K, D, U), BF16),
            pltpu.VMEM((D, VH), BF16),
            pltpu.VMEM((2 * R, D), BF16),
            pltpu.VMEM((D, 2 * R), BF16),
            pltpu.VMEM((2 * R, VH), BF16),
            pltpu.VMEM((NC, 8, 256, C), BF16),
            pltpu.VMEM((NC, 2, 256, C), BF16),
            pltpu.VMEM((NC, 2, 2, 256, C), BF16),
            pltpu.VMEM((2, 2, 4, 4, 2 * T, U), BF16),
            pltpu.VMEM((2, 4, 4, 2 * T, U), BF16),
            pltpu.VMEM((2, 2, 2, 2 * T, U), BF16),
            pltpu.VMEM((2, 2, 2, 2, 2 * T, U), BF16),
            pltpu.VMEM((2, 2, T, U), BF16),
            pltpu.VMEM((2, 2, 2, T, U), BF16),
            pltpu.VMEM((2 * T, D), BF16),
            pltpu.VMEM((4, T, 512), BF16),
            pltpu.VMEM((512, 4 * T), BF16),
            pltpu.VMEM((5, T, U), BF16),
            pltpu.VMEM((5, 4 * T, U), BF16),
            pltpu.VMEM((K, 256, U), BF16),
            pltpu.VMEM((K, 256, U), BF16),
            pltpu.VMEM((K, 256), F32),
            pltpu.VMEM((K, 256), F32),
            pltpu.VMEM((16, T, U), BF16),
            pltpu.VMEM((16, T, U), BF16),
            pltpu.VMEM((2, 16, T), F32),
            pltpu.VMEM((2 * R, 128), F32),
            pltpu.VMEM((2 * R, 128), F32),
            pltpu.VMEM((2 * R, 128), F32),
            pltpu.VMEM((32, 8, T), F32),
            pltpu.VMEM((2 * R, C), F32),
            pltpu.VMEM((T, U), BF16),
            pltpu.VMEM((K, 256), F32),
            pltpu.VMEM((K, 256, U), BF16),
            dma((3,)),
            dma((2,)),
            dma((2,)),
            dma((2,)),
            dma((3,)),
            dma((72,)),
            dma((72,)),
            dma((4,)),
            dma((4,)),
            dma((32,)),
            dma((32,)),
            dma((6 * NC,)),
            dma((6 * NC,)),
            dma((NC,)),
            dma((NC,)),
            dma((NC,)),
            dma((2,)),
            dma((2,)),
            dma((12,)),
            dma((12,)),
            dma((12,)),
            dma((12,)),
            dma((16,)),
            dma((16,)),
            dma((4,)),
            dma((4,)),
        ],
        compiler_params=pltpu.CompilerParams(
            collective_id=0, has_side_effects=True, vmem_limit_bytes=67043328
        ),
    )(
        mix_weight.T,
        saved_lse.T,
        loss_scale[None, :],
        targets[None, :],
        hidden,
        proj_weight,
        out_weight,
    )
    gh, gm, gp, go = pl.pallas_call(
        place,
        out_shape=outs,
        in_specs=[hbm] * 4,
        out_specs=(hbm,) * 4,
        scratch_shapes=[pltpu.VMEM(o.shape, o.dtype) for o in outs] + [dma((7,)), dma((7,))],
    )(*found)
    return gh, gm.T, gp, go


def solution(mesh):
    finer = Mesh(mesh.devices.reshape(4, 2, 2, 4, 2), AXES)
    in_specs = (
        P(DP, None),
        P(),
        P(None, None, VOC),
        P(None, VOC),
        P(DP, None),
        P(DP),
        P(DP),
    )
    out_specs = (P(DP, VOC), P(DP, None), P(None, DP, VOC), P(DP, VOC))
    return jax.shard_map(
        shards, mesh=finer, in_specs=in_specs, out_specs=out_specs, check_vma=False
    )
```

time: 429 us -> 142 us (0.33)
  waiting for transfers between devices: 317 us -> 0 us
  Pallas kernels: 0 us -> 141 us
  matrix products: 54.3 us -> 0 us
  local copies, waits for them, and re-layouts: 19.9 us -> 0 us
  starting transfers between devices: 19.2 us -> 0 us
  between operations: 14.1 us -> 0.8 us
    reduce_scatter x2 -> x0, waiting for transfers between devices: 153 us -> none  [sum_by_axis(): subtotal = lax.psum_scatter(subtotal, axis, scatter_dimension=0, tiled=True)]
    pallas_call x0 -> x2, Pallas kernels: none -> 141 us  [the longest x1 138 us: shards(): pl.pallas_call(kernel, out_shape=outs, in_specs=[vm, vm, vm, vm, hbm, hbm...]
    unnamed x5 -> x0, waiting for transfers between devices: 68.4 us -> none
    dot_general x9 -> x0, matrix products: 54.3 us -> none  [the longest x1 16.7 us: shards(): lax.dot_general(part_rows, grad_logits, (((1,), (1,)), ((), ())), preferr...]
    all_gather x1 -> x0, waiting for transfers between devices: 52.5 us -> none  [shards(): comp_all = lax.all_gather(comp_local, 'vocab', axis=2, tiled=True)]
    all_to_all x4 -> x0, waiting for transfers between devices: 43.5 us -> none  [the longest x3 36.8 us: sum_at_owner(): parts = lax.all_to_all(in_blocks(array, dim, count), axis, 0, 0, tiled=True)]
    all_to_all x4 -> x0, starting transfers between devices: 18.9 us -> none  [the longest x3 15 us: sum_at_owner(): parts = lax.all_to_all(in_blocks(array, dim, count), axis, 0, 0, tiled=True)]
    unnamed x36 -> x0, local copies, waits for them, and re-layouts: 7.55 us -> none
  transfers between devices with their start and end apart: 8 -> 0, of which waited for: 7 -> 0; matrix products, arithmetic and copies ran while one was open for 8% -> 0% of each run, Pallas kernels for 0% -> 0%
where the time goes in v1:
time: 142 us; the launch traced here: 141 us
  Pallas kernels  141 us (99%)
    pallas_call x1, Pallas kernels, shards(): pl.pallas_call(kernel, out_shape=outs, in_specs=[vm, vm, vm, vm, hbm, hbm...  138 us

profile of v1, /device:TPU:1, one launch (start us, length us, event | category | flops | bytes accessed | tf_op | source)
XLA Modules:
  0.0 141.4 jit_solution(13807789396142510618)
XLA Ops:
  0.6 138.0 %shard_map.102 = (bf16[128,128]{1,0:T(8,128)(2,1)}, f32[4,256]{1,0:T(4,128)}, bf16[4,256,128]{2,1,0:T(8,128)(2,1)}, bf16[256,4096]{1,0:T(8,128)(2,1)}) custom-call(bf16[4,2048]{1,0:T(4,128)(2,1)} %bitcast.5, f32[4,128]{1,0:T(4,128)} %bitcast.6, f32[1,128]{1,0:T(1,128)} %bitcast.7, s32[1,128]{1,0:T(1,128)} %bitcast.8, bf16[128,2048]{1,0:T(8,128)(2,1)} %hidden_hbm.1, ...), custom_call_target="tpu_custom_call" | custom-call | tf_op jit(solution)/shard_map/pallas_call | solution.py:777
  138.7 2.6 %shard_map.103 = (bf16[128,128]{1,0:T(8,128)(2,1)}, f32[4,256]{1,0:T(4,128)}, bf16[4,256,128]{2,1,0:T(8,128)(2,1)}, bf16[256,4096]{1,0:T(8,128)(2,1)}) custom-call(bf16[128,128]{1,0:T(8,128)(2,1)} %get-tuple-element.12.gh, f32[4,256]{1,0:T(4,128)} %get-tuple-element.13.gm, bf16[4,256,128]{2,1,0:T(8,128)(2,1)} %get-tuple-element.14.gp, ...), custom_call_target="tpu_custom_call" | custom-call | tf_op jit(solution)/shard_map/pallas_call | solution.py:857

commit v2 on v1

--- a/solution.py
+++ b/solution.py
@@ -24,6 +24,7 @@
 VH = VL // 2
 NC = 8
 C = VH // NC
+W2 = 2 * C
 
 
 def nt(a, b):
@@ -200,25 +201,30 @@
         return dev(y_=a_, z_=b_) if col == 0 else dev(z_=a_, y_=b_)
 
     def ag_copy(col, i, ref, to):
-        return rc(ref, ref, ag_s.at[col * 36 + i], ag_r.at[col * 36 + i], to)
-
-    ag_sent = []
+        r = 30 + i if col is None else col * 15 + i
+        return rc(ref, ref, ag_s, ag_r.at[r], to)
 
     def ag_send(col, i, ref, to):
-        cp = ag_copy(col, i, ref, to)
-        cp.start()
-        ag_sent.append(cp)
+        ag_copy(col, i, ref, to).start()
 
     def ag_wait(col, i, ref):
         ag_copy(col, i, ref, partner_c).wait_recv()
 
     def second(col, i, ref):
         a, b = pos(col)
-        ag_send(col, 4 + 4 * i, ref, dev_ab(col, a, m4(b + 1)))
-        ag_send(col, 4 + 4 * i + 1, ref, dev_ab(col, a, m4(b - 1)))
-
-    def across(col, i, j, ref):
-        ag_send(col, 20 + i * 4 + j, ref, partner_c)
+        ag_send(col, 3 + 3 * i, ref, dev_ab(col, a, m4(b + 1)))
+        ag_send(col, 3 + 3 * i + 1, ref, dev_ab(col, a, m4(b - 1)))
+
+    def across(i, ref):
+        ag_send(None, i, ref, partner_c)
+
+    def flip(col, a_, b_, c_):
+        z_, y_ = (b_, a_) if col == 0 else (a_, b_)
+        row = pl.multiple_of(lax.rem(z_, 2) * R + col * 2 * T, 2 * T)
+        lane = pl.multiple_of((lax.div(z_, 2) * 8 + y_ * 2 + c_) * U, U)
+        comp_t[pl.ds(lane, U), pl.ds(row, 2 * T)] = jnp.transpose(
+            comp[pl.ds(row, 2 * T), pl.ds(lane, U)]
+        )
 
     proj_copy.wait()
     for k in range(K):
@@ -237,16 +243,12 @@
         a, b = pos(col)
         own = at_ab(col, a, b, c)
         second(col, 0, own)
-        across(col, 0, 0, own)
+        across(0, own)
 
     def hs_copy(i):
         p = m4(x + (0, 1, -1, 2)[i])
         return rc(
-            hidden.at[:, pl.ds(pl.multiple_of(p * 512, 512), 512)],
-            hs.at[i],
-            hs_s.at[i],
-            hs_r.at[i],
-            dev(x_=p),
+            hidden.at[:, pl.ds(pl.multiple_of(p * 512, 512), 512)], hs.at[i], hs_s, hs_r, dev(x_=p)
         )
 
     for i in range(1, 4):
@@ -275,49 +277,54 @@
         ag_wait(col, 0, at_ab(col, prev, b, c))
         ag_send(col, 2, at_ab(col, prev, b, c, 0, T), dev_ab(col, nxt, b))
         second(col, 1, at_ab(col, prev, b, c))
-        across(col, 1, 0, at_ab(col, prev, b, c))
+        across(1, at_ab(col, prev, b, c))
         ag_wait(col, 1, at_ab(col, nxt, b, c))
-        ag_send(col, 3, at_ab(col, nxt, b, c, T, T), dev_ab(col, prev, b))
+        ag_send(col, 2, at_ab(col, nxt, b, c, T, T), dev_ab(col, prev, b))
         second(col, 2, at_ab(col, nxt, b, c))
-        across(col, 2, 0, at_ab(col, nxt, b, c))
+        across(2, at_ab(col, nxt, b, c))
     info_in = rc(info2.at[1 - zl], info2.at[1 - zl], sem_i.at[0], sem_i.at[1], partner_z)
     info_in.wait_recv()
     row_columns(1 - zl)
-    w_copy.wait()
-    lax.fori_loop(0, 4, pick, 0)
     for col in range(2):
         a, b = pos(col)
         far = m4(a + 2)
-        ag_wait(col, 2, at_ab(col, far, b, c, 0, T))
-        ag_wait(col, 3, at_ab(col, far, b, c, T, T))
+        ag_wait(col, 2, at_ab(col, far, b, c))
         second(col, 3, at_ab(col, far, b, c))
-        across(col, 3, 0, at_ab(col, far, b, c))
+        across(3, at_ab(col, far, b, c))
+    w_copy.wait()
+    lax.fori_loop(0, 4, pick, 0)
     for i in range(4):
         for col in range(2):
             a, b = pos(col)
             a_ = m4(a + (0, -1, 1, 2)[i])
             prev, nxt = m4(b - 1), m4(b + 1)
-            ag_wait(col, 4 + 4 * i, at_ab(col, a_, prev, c))
-            ag_send(col, 4 + 4 * i + 2, at_ab(col, a_, prev, c, 0, T), dev_ab(col, a, nxt))
-            across(col, i, 1, at_ab(col, a_, prev, c))
-            ag_wait(col, 4 + 4 * i + 1, at_ab(col, a_, nxt, c))
-            ag_send(col, 4 + 4 * i + 3, at_ab(col, a_, nxt, c, T, T), dev_ab(col, a, prev))
-            across(col, i, 2, at_ab(col, a_, nxt, c))
+            ag_wait(col, 3 + 3 * i, at_ab(col, a_, prev, c))
+            ag_send(col, 3 + 3 * i + 2, at_ab(col, a_, prev, c, 0, T), dev_ab(col, a, nxt))
+            across(i, at_ab(col, a_, prev, c))
+            ag_wait(col, 3 + 3 * i + 1, at_ab(col, a_, nxt, c))
+            ag_send(col, 3 + 3 * i + 2, at_ab(col, a_, nxt, c, T, T), dev_ab(col, a, prev))
+            across(i, at_ab(col, a_, nxt, c))
+            for b_ in (b, prev, nxt):
+                flip(col, a_, b_, c)
     for i in range(4):
         for col in range(2):
             a, b = pos(col)
             a_ = m4(a + (0, -1, 1, 2)[i])
             far = m4(b + 2)
-            ag_wait(col, 4 + 4 * i + 2, at_ab(col, a_, far, c, 0, T))
-            ag_wait(col, 4 + 4 * i + 3, at_ab(col, a_, far, c, T, T))
-            across(col, i, 3, at_ab(col, a_, far, c))
+            ag_wait(col, 3 + 3 * i + 2, at_ab(col, a_, far, c))
+            across(i, at_ab(col, a_, far, c))
+            flip(col, a_, far, c)
     for i in range(4):
-        for j in range(4):
-            for col in range(2):
-                a, b = pos(col)
-                a_ = m4(a + (0, -1, 1, 2)[i])
-                b_ = m4(b + (0, -1, 1, 2)[j])
-                ag_wait(col, 20 + i * 4 + j, at_ab(col, a_, b_, 1 - c))
+        ag_wait(None, i, comp.at[pl.ds(0, T), :])
+        for col in range(2):
+            a, b = pos(col)
+            a_ = m4(a + (0, -1, 1, 2)[i])
+
+            def flip_step(b_, carry):
+                flip(col, a_, b_, 1 - c)
+                return carry
+
+            lax.fori_loop(0, 4, flip_step, 0)
 
     lane_t = lax.broadcasted_iota(jnp.int32, (T, 128), 1)
     acc = jnp.zeros((T, 128), F32)
@@ -334,7 +341,7 @@
     tl[0] = jnp.transpose(acc)[0:8]
 
     def tl_copy(o):
-        return rc(tl.at[0], tl.at[o], tl_s.at[o], tl_r.at[o], mate(o))
+        return rc(tl.at[0], tl.at[o], tl_s, tl_r, mate(o))
 
     def tl_start(o, carry):
         tl_copy(o).start()
@@ -342,22 +349,14 @@
 
     lax.fori_loop(1, 32, tl_start, 0)
 
-    def flip(n, carry):
-        cols = pl.ds(pl.multiple_of(n * U, U), U)
-        for m in range(2):
-            comp_t[cols, pl.ds(m * R, R)] = jnp.transpose(comp[pl.ds(m * R, R), cols])
-        return carry
-
-    lax.fori_loop(0, D // U, flip, 0)
-
     lane_w = lax.broadcasted_iota(jnp.int32, (2 * T, 128), 1).astype(F32)
 
-    def chunk_logits(cc, m, put):
+    def block_logits(p, m, put):
         rows = pl.ds(pl.multiple_of(m * 2 * T, 2 * T), 2 * T)
-        logit = nn(comp[rows, :], w[:, pl.ds(pl.multiple_of(cc * C, C), C)])
-        shift = jnp.asarray(cc * C, F32)
+        logit = nn(comp[rows, :], w[:, pl.ds(pl.multiple_of(p * W2, W2), W2)])
+        shift = jnp.asarray(p * W2, F32)
         lse_m, tgt_m = lsec[rows, :], tgtc[rows, :] - shift
-        for e in range(C // 128):
+        for e in range(W2 // 128):
             prob = jnp.exp(logit[:, e * 128 : (e + 1) * 128] - lse_m)
             hot = jnp.where(lane_w + float(e * 128) == tgt_m, 1.0, 0.0)
             put(rows, e, prob - hot)
@@ -366,16 +365,13 @@
         def put(rows, e, val):
             pbuf[rows, pl.ds(e * 128, 128)] = val
 
-        chunk_logits(0, m, put)
+        block_logits(0, m, put)
         return carry
 
     lax.fori_loop(0, 4, hold, 0)
 
-    def tl_wait(o, carry):
-        tl_copy(o).wait()
-        return carry
-
-    lax.fori_loop(1, 32, tl_wait, 0)
+    tl_all = rc(tl.at[pl.ds(1, 31)], tl.at[pl.ds(1, 31)], tl_s, tl_r, partner_c)
+    tl_all.wait_recv()
     target_logit = jnp.sum(tl[...], axis=0)
     coef_rows = []
     gml_rows = []
@@ -402,15 +398,15 @@
         gml = jnp.where(lane_t == K + k, mine - high, gml)
     gpx[4] = gml.astype(BF16)
 
-    def ring(idx, n, piece, me, right, left, r1, rf, ss, rs):
+    def ring(piece, me, right, left, r1, rf, ss, r1_sem, rf_sem, r1_all, rf_all):
         two, one, back = m4(me + 2), m4(me + 1), m4(me - 1)
         copies = (
-            lambda: rc(piece(two, 0), r1(0), ss.at[idx], rs.at[idx], right),
-            lambda: rc(piece(one, 1), rf(0, 1), ss.at[idx + 1], rs.at[idx + 1], right),
-            lambda: rc(piece(two, 1), r1(1), ss.at[idx + 2], rs.at[idx + 2], left),
-            lambda: rc(piece(back, 0), rf(1, 0), ss.at[idx + 3], rs.at[idx + 3], left),
-            lambda: rc(piece(one, 0), rf(0, 0), ss.at[idx + 4], rs.at[idx + 4], right),
-            lambda: rc(piece(back, 1), rf(1, 1), ss.at[idx + 5], rs.at[idx + 5], left),
+            lambda: rc(piece(two, 0), r1(0), ss, r1_sem, right),
+            lambda: rc(piece(one, 1), rf(0, 1), ss, rf_sem, right),
+            lambda: rc(piece(two, 1), r1(1), ss, r1_sem, left),
+            lambda: rc(piece(back, 0), rf(1, 0), ss, rf_sem, left),
+            lambda: rc(piece(one, 0), rf(0, 0), ss, rf_sem, right),
+            lambda: rc(piece(back, 1), rf(1, 1), ss, rf_sem, left),
         )
 
         def first(which=(0, 2, 1, 3)):
@@ -421,29 +417,21 @@
             ref[...] = (ref[...].astype(F32) + other[...].astype(F32)).astype(BF16)
 
         def forward():
-            copies[0]().wait_recv()
+            rc(r1_all, r1_all, ss, r1_sem, right).wait_recv()
             add(piece(one, 0), r1(0))
             copies[4]().start()
-            copies[2]().wait_recv()
             add(piece(back, 1), r1(1))
             copies[5]().start()
 
         def arrive():
-            for i in (1, 3, 4, 5):
-                copies[i]().wait_recv()
-
-        def drain():
-            for i in range(6):
-                copies[i]().wait_send()
-
-        return first, forward, arrive, drain
+            rc(rf_all, rf_all, ss, rf_sem, right).wait_recv()
+
+        return first, forward, arrive
 
     x_right, x_left = dev(x_=m4(x + 1)), dev(x_=m4(x - 1))
 
     def x_ring(cc):
         return ring(
-            cc * 6,
-            6,
             lambda t, h: part.at[cc, t * 2 + h],
             x,
             x_right,
@@ -451,47 +439,47 @@
             lambda i: r1x.at[cc, i],
             lambda i, h: rfx.at[cc, i, h],
             x_s,
-            x_r,
-        )
-
-    def chunk_out(cc):
-        cols = pl.ds(pl.multiple_of(cc * C, C), C)
-        for i in range(4):
-            t = m4(x + (2, 1, -1, 0)[i])
-            rows = pl.ds(pl.multiple_of(t * 512, 512), 512)
+            x_r.at[2 * cc],
+            x_r.at[2 * cc + 1],
+            r1x.at[cc],
+            rfx.at[cc],
+        )
+
+    def grad_out(p):
+        cols = pl.ds(p * W2, W2)
+        order = ((2, 0), (2, 1), (1, 1), (-1, 0), (1, 0), (-1, 1), (0, 0), (0, 1))
+        for i, (step, h) in enumerate(order):
+            t = m4(x + step)
+            rows = pl.ds(pl.multiple_of(t * 512 + h * 256, 256), 256)
             res = nn(comp_t[rows, :], gl[:, cols]).astype(BF16)
-            part[cc, t * 2] = res[0:256]
-            part[cc, t * 2 + 1] = res[256:512]
-            if i < 3:
-                x_ring(cc)[0](((0, 2), (1,), (3,))[i])
+            for e in range(2):
+                part[2 * p + e, t * 2 + h] = res[:, e * C : (e + 1) * C]
+            if i < 4:
+                for e in range(2):
+                    x_ring(2 * p + e)[0](((0, 2, 1, 3)[i],))
 
     def scale_first(m, carry):
         rows = pl.ds(pl.multiple_of(m * 2 * T, 2 * T), 2 * T)
         coef_m = coefc[rows, :]
-        for e in range(C // 128):
+        for e in range(W2 // 128):
             gl[rows, pl.ds(e * 128, 128)] = (coef_m * pbuf[rows, pl.ds(e * 128, 128)]).astype(BF16)
         return carry
 
     lax.fori_loop(0, 4, scale_first, 0)
-    chunk_out(0)
-
-    def chunk(cc, carry):
-        def rows_of(m, carry2):
+
+    def grad_logits(p):
+        def rows_of(m, carry):
             coef_m = coefc[pl.ds(pl.multiple_of(m * 2 * T, 2 * T), 2 * T), :]
 
             def put(rows, e, val):
-                gl[rows, pl.ds(pl.multiple_of(cc * C + e * 128, 128), 128)] = (coef_m * val).astype(
+                gl[rows, pl.ds(pl.multiple_of(p * W2 + e * 128, 128), 128)] = (coef_m * val).astype(
                     BF16
                 )
 
-            chunk_logits(cc, m, put)
-            return carry2
+            block_logits(p, m, put)
+            return carry
 
         lax.fori_loop(0, 4, rows_of, 0)
-        chunk_out(cc)
-        return carry
-
-    lax.fori_loop(1, NC, chunk, 0)
 
     def comp_grad(col):
         def tile(i, carry):
@@ -518,8 +506,6 @@
         me = z if col == 0 else y
         mk = (lambda p: dev(z_=p)) if col == 0 else (lambda p: dev(y_=p))
         return ring(
-            col * 6,
-            6,
             lambda t, h: gcb.at[c, col, t, pl.ds(2 * h, 2)],
             me,
             mk(m4(me + 1)),
@@ -527,7 +513,10 @@
             lambda i: r1a.at[col, i],
             lambda i, h: rfa.at[col, i, h],
             a_s,
-            a_r,
+            a_r.at[2 * col],
+            a_r.at[2 * col + 1],
+            r1a.at[col],
+            rfa.at[col],
         )
 
     def b_ring(col):
@@ -535,8 +524,6 @@
         me = y if col == 0 else z
         mk = (lambda p: dev(y_=p)) if col == 0 else (lambda p: dev(z_=p))
         return ring(
-            col * 6,
-            6,
             lambda t, h: gcb.at[c, col, first, t, pl.ds(h * T, T)],
             me,
             mk(m4(me + 1)),
@@ -544,7 +531,10 @@
             lambda i: r1b.at[col, i],
             lambda i, h: rfb.at[col, i, h],
             b_s,
-            b_r,
+            b_r.at[2 * col],
+            b_r.at[2 * col + 1],
+            r1b.at[col],
+            rfb.at[col],
         )
 
     def merge(col, swap):
@@ -585,38 +575,11 @@
         cols = pl.ds(pl.multiple_of(zl * VH + cc * C, C), C)
         dst = go_out.at[:, cols]
         return (
-            rc(part.at[cc, x * 2 + 1 - zl], dst, zx_s.at[cc], zx_r.at[cc], partner_z),
-            pltpu.make_async_copy(part.at[cc, x * 2 + zl], dst, zx_l.at[cc]),
-        )
-
-    for cc in range(4):
-        x_ring(cc)[1]()
-    swap0 = comp_grad(0)
-    x_ring(4)[1]()
-    swap1 = comp_grad(1)
-    x_ring(5)[1]()
-    merge(0, swap0)
-    a_ring(0)[0]()
-    merge(1, swap1)
-    a_ring(1)[0]()
-    a_ring(0)[1]()
-    a_ring(1)[1]()
-    for i in range(1, 4):
-        hs_copy(i).wait()
-    for i in range(4):
-        hst[:, pl.ds(i * T, T)] = jnp.transpose(hs[i])
-    x_ring(6)[1]()
-    a_ring(0)[2]()
-    finish_a(0)
-    b_ring(0)[0]()
-    a_ring(1)[2]()
-    finish_a(1)
-    b_ring(1)[0]()
-    b_ring(0)[1]()
-    b_ring(1)[1]()
-    x_finish(0)
-
-    for col in range(2):
+            rc(part.at[cc, x * 2 + 1 - zl], dst, zx_s, zx_r, partner_z),
+            pltpu.make_async_copy(part.at[cc, x * 2 + zl], dst, zx_l),
+        )
+
+    def finish_b(col):
         first = z if col == 0 else y
         me = y if col == 0 else z
         b_ring(col)[2]()
@@ -632,23 +595,59 @@
             ].astype(F32)
             gpx[k] = (total * (1.0 - cf * cf)).astype(BF16)
 
+    grad_out(0)
+    grad_logits(1)
+    grad_out(1)
+    x_ring(0)[1]()
+    grad_logits(2)
+    grad_logits(3)
+    x_ring(1)[1]()
+    swap0 = comp_grad(0)
+    grad_out(2)
+    merge(0, swap0)
+    a_ring(0)[0]()
+    x_ring(2)[1]()
+    swap1 = comp_grad(1)
+    a_ring(0)[1]()
+    x_ring(3)[1]()
+    grad_out(3)
+    merge(1, swap1)
+    a_ring(1)[0]()
+    x_finish(0)
+    a_ring(0)[2]()
+    finish_a(0)
+    b_ring(0)[0]()
+    a_ring(1)[1]()
+    hs_all = rc(hs.at[pl.ds(1, 3)], hs.at[pl.ds(1, 3)], hs_s, hs_r, partner_c)
+    hs_all.wait_recv()
+    for i in range(4):
+        hst[:, pl.ds(i * T, T)] = jnp.transpose(hs[i])
+    b_ring(0)[1]()
+    x_finish(1)
+    a_ring(1)[2]()
+    finish_a(1)
+    b_ring(1)[0]()
+    finish_b(0)
+    b_ring(1)[1]()
+    finish_b(1)
+
     def slot(i, r0=0, n=T):
         return gpall.at[:, pl.ds(i * T + r0, n)]
 
     g_copies = (
-        rc(gpx, slot(1), g_s.at[0], g_r.at[0], x_right),
-        rc(gpx, slot(2), g_s.at[1], g_r.at[1], x_left),
-        rc(slot(1, 0, T // 2), slot(3, 0, T // 2), g_s.at[2], g_r.at[2], x_right),
-        rc(slot(2, T // 2, T // 2), slot(3, T // 2, T // 2), g_s.at[3], g_r.at[3], x_left),
+        rc(gpx, slot(1), g_s, g_r.at[0], x_right),
+        rc(gpx, slot(2), g_s, g_r.at[1], x_left),
+        rc(slot(1, 0, T // 2), slot(3, 0, T // 2), g_s, g_r.at[2], x_right),
+        rc(slot(2, T // 2, T // 2), slot(3, T // 2, T // 2), g_s, g_r.at[2], x_left),
     )
     g_copies[0].start()
     g_copies[1].start()
-    x_ring(7)[1]()
+    x_ring(4)[1]()
 
     def h_copy(o):
         p = lax.rem(v + o, 16)
         to = (x, zl, lax.div(p, 8), lax.rem(lax.div(p, 2), 4), lax.rem(p, 2))
-        return rc(hts.at[o], hrecv.at[o], h_s.at[o], h_r.at[o], to)
+        return rc(hts.at[o], hrecv.at[o], h_s, h_r, to)
 
     def h_tile(o):
         p = lax.rem(v + o, 16)
@@ -666,19 +665,11 @@
     lax.fori_loop(1, 16, h_step, 0)
     hrecv[0] = h_tile(0).astype(BF16)
     gpall[:, pl.ds(0, T)] = gpx[...]
-    x_finish(1)
+    x_ring(5)[1]()
     x_finish(2)
     x_finish(3)
-    g_copies[0].wait_recv()
-    g_copies[2].start()
-    g_copies[1].wait_recv()
-    g_copies[3].start()
-
-    def h_wait(o, carry):
-        h_copy(o).wait()
-        return carry
-
-    lax.fori_loop(1, 16, h_wait, 0)
+    h_all = rc(hts.at[pl.ds(1, 15)], hrecv.at[pl.ds(1, 15)], h_s, h_r, partner_c)
+    h_all.wait_recv()
     mw = jnp.concatenate(
         [mix_t[:, pl.ds(own_cols, U)].astype(F32)] * 2 + [jnp.zeros((120, U), F32)], axis=0
     ).astype(BF16)
@@ -692,11 +683,16 @@
         pltpu.make_async_copy(gm_v, gm_out, sem_o.at[2]),
     )
     out_copies[0].start()
+    x_ring(6)[1]()
+    g_copies[0].wait_recv()
+    g_copies[2].start()
+    g_copies[1].wait_recv()
+    g_copies[3].start()
+    x_ring(7)[1]()
     x_finish(4)
     x_finish(5)
 
-    g_copies[2].wait_recv()
-    g_copies[3].wait_recv()
+    rc(slot(3), slot(3), g_s, g_r.at[2], x_right).wait_recv()
 
     def product(half, k):
         return nn(hst[pl.ds(pl.multiple_of(half * 256, 256), 256), :], gpall[k])
@@ -729,21 +725,20 @@
     out_copies[1].start()
     out_copies[2].start()
 
-    for cp in ag_sent:
+    for cp in (info_copy, swap0, swap1, *p_copies, tl_all, hs_all, h_all):
         cp.wait_send()
-    for cp in (info_copy, swap0, swap1, *g_copies, *p_copies):
-        cp.wait_send()
-    for col in range(2):
-        a_ring(col)[3]()
-        b_ring(col)[3]()
-
-    def x_drain(cc, carry):
-        x_ring(cc)[3]()
-        for cp in z_copies(cc):
-            cp.wait()
-        return carry
-
-    lax.fori_loop(0, NC, x_drain, 0)
+    for ref, sem in (
+        (comp.at[pl.ds(0, 992), :], ag_s),
+        (part.at[pl.ds(0, 6)], x_s),
+        (part.at[0], zx_s),
+        (gcb.at[0, :, pl.ds(0, 3)], a_s),
+        (gcb.at[0, 0, pl.ds(0, 3), pl.ds(0, 2)], b_s),
+        (gpall.at[:, pl.ds(0, 3 * T)], g_s),
+    ):
+        rc(ref, ref, sem, zx_r, partner_z).wait_send()
+    half_out = go_out.at[:, pl.ds(0, VH)]
+    rc(half_out, half_out, zx_s, zx_r, partner_z).wait_recv()
+    pltpu.make_async_copy(part.at[0], part.at[0], zx_l).wait()
     for cp in out_copies:
         cp.wait()
 
@@ -811,7 +806,7 @@
             pltpu.VMEM((2 * R, 128), F32),
             pltpu.VMEM((2 * R, 128), F32),
             pltpu.VMEM((32, 8, T), F32),
-            pltpu.VMEM((2 * R, C), F32),
+            pltpu.VMEM((2 * R, W2), F32),
             pltpu.VMEM((T, U), BF16),
             pltpu.VMEM((K, 256), F32),
             pltpu.VMEM((K, 256, U), BF16),
@@ -820,27 +815,27 @@
             dma((2,)),
             dma((2,)),
             dma((3,)),
-            dma((72,)),
-            dma((72,)),
-            dma((4,)),
-            dma((4,)),
-            dma((32,)),
-            dma((32,)),
-            dma((6 * NC,)),
-            dma((6 * NC,)),
-            dma((NC,)),
-            dma((NC,)),
-            dma((NC,)),
+            dma,
+            dma((34,)),
+            dma,
+            dma,
+            dma,
+            dma,
+            dma,
+            dma((16,)),
+            dma,
+            dma,
+            dma,
             dma((2,)),
             dma((2,)),
-            dma((12,)),
-            dma((12,)),
-            dma((12,)),
-            dma((12,)),
-            dma((16,)),
-            dma((16,)),
+            dma,
             dma((4,)),
+            dma,
             dma((4,)),
+            dma,
+            dma,
+            dma,
+            dma((3,)),
         ],
         compiler_params=pltpu.CompilerParams(
             collective_id=0, has_side_effects=True, vmem_limit_bytes=67043328

time: 142 us -> 126 us (0.89)
  Pallas kernels: 141 us -> 124 us
    pallas_call x1, Pallas kernels: 138 us -> 121 us  [shards(): pl.pallas_call(kernel, out_shape=outs, in_specs=[vm, vm, vm, vm, hbm, hbm...]
where the time goes in v2:
time: 126 us; the launch traced here: 125 us
  Pallas kernels  124 us (98%)
    pallas_call x1, Pallas kernels, shards(): pl.pallas_call(kernel, out_shape=outs, in_specs=[vm, vm, vm, vm, hbm, hbm...  121 us
    pallas_call x1, Pallas kernels, shards(): pl.pallas_call(place, out_shape=outs, in_specs=[hbm] * 4, out_specs=(hbm,...  2.57 us

profile of v2, /device:TPU:1, one launch (start us, length us, event | category | flops | bytes accessed | tf_op | source)
XLA Modules:
  0.0 124.7 jit_solution(13071013532020447734)
XLA Ops:
  0.6 121.3 %shard_map.102 = (bf16[128,128]{1,0:T(8,128)(2,1)}, f32[4,256]{1,0:T(4,128)}, bf16[4,256,128]{2,1,0:T(8,128)(2,1)}, bf16[256,4096]{1,0:T(8,128)(2,1)}) custom-call(bf16[4,2048]{1,0:T(4,128)(2,1)} %bitcast.5, f32[4,128]{1,0:T(4,128)} %bitcast.6, f32[1,128]{1,0:T(1,128)} %bitcast.7, s32[1,128]{1,0:T(1,128)} %bitcast.8, bf16[128,2048]{1,0:T(8,128)(2,1)} %hidden_hbm.1, ...), custom_call_target="tpu_custom_call" | custom-call | tf_op jit(solution)/shard_map/pallas_call | solution.py:772
  122.0 2.6 %shard_map.103 = (bf16[128,128]{1,0:T(8,128)(2,1)}, f32[4,256]{1,0:T(4,128)}, bf16[4,256,128]{2,1,0:T(8,128)(2,1)}, bf16[256,4096]{1,0:T(8,128)(2,1)}) custom-call(bf16[128,128]{1,0:T(8,128)(2,1)} %get-tuple-element.12.gh, f32[4,256]{1,0:T(4,128)} %get-tuple-element.13.gm, bf16[4,256,128]{2,1,0:T(8,128)(2,1)} %get-tuple-element.14.gp, ...), custom_call_target="tpu_custom_call" | custom-call | tf_op jit(solution)/shard_map/pallas_call | solution.py:852

commit v3 on v2

--- a/solution.py
+++ b/solution.py
@@ -60,13 +60,13 @@
     rd,
     r1a,
     rfa,
-    r1b,
     rfb,
     wt,
     hs,
     hst,
     gpx,
     gpall,
+    gmla,
     prods,
     prodr,
     gms,
@@ -108,6 +108,8 @@
     h_r,
     g_s,
     g_r,
+    gm_s,
+    gm_r,
 ):
     x = lax.axis_index("x")
     zl = lax.axis_index("zl")
@@ -139,23 +141,6 @@
     partner_c = dev(c_=1 - c)
     partner_z = (x, 1 - zl, zh, y, c)
 
-    q32 = z * 8 + y * 2 + c
-
-    def mate(o):
-        p = lax.rem(q32 + o, 32)
-        zz = lax.div(p, 8)
-        return (x, lax.rem(zz, 2), lax.div(zz, 2), lax.rem(lax.div(p, 2), 4), lax.rem(p, 2))
-
-    barrier = pltpu.get_barrier_semaphore()
-
-    def greet(o, carry):
-        pl.semaphore_signal(barrier, inc=1, device_id=mate(o), device_id_type=MESH_ID)
-        return carry
-
-    lax.fori_loop(1, 32, greet, 0)
-    for o in range(1, 4):
-        pl.semaphore_signal(barrier, inc=1, device_id=dev(x_=m4(x + o)), device_id_type=MESH_ID)
-
     hidden_copy = pltpu.make_async_copy(hidden_hbm, hidden, sem_w.at[0])
     proj_copy = pltpu.make_async_copy(proj_hbm, proj, sem_w.at[1])
     w_copy = pltpu.make_async_copy(
@@ -164,24 +149,23 @@
     hidden_copy.start()
     proj_copy.start()
     w_copy.start()
-    hidden_copy.wait()
-    mix_logits = nt(mix_t[...], hidden[...])
-    info2[zl, 0:4] = lse_t[...]
-    info2[zl, 4:8] = mix_logits - jnp.log(jnp.sum(jnp.exp(mix_logits), axis=0, keepdims=True))
-    info2[zl, 8:9] = scale[...]
-    info2[zl, 9:10] = target[...].astype(F32)
-    info2[zl, 10:16] = jnp.zeros((6, T), F32)
-
-    def row_columns(g):
-        cols = jnp.transpose(jnp.concatenate([info2[g], jnp.zeros((112, T), F32)], axis=0))
-        local = cols[:, 9:10] - (v * VL + zl * VH).astype(F32)
-        for k in range(K):
-            rows = pl.ds(pl.multiple_of(g * R + k * T, T), T)
-            lsec[rows, :] = jnp.broadcast_to(cols[:, k : k + 1], (T, 128))
-            tgtc[rows, :] = jnp.broadcast_to(local, (T, 128))
-
-    row_columns(zl)
-    info_copy = rc(info2.at[zl], info2.at[zl], sem_i.at[0], sem_i.at[1], partner_z)
+
+    q32 = z * 8 + y * 2 + c
+
+    def mate(o):
+        p = lax.rem(q32 + o, 32)
+        zz = lax.div(p, 8)
+        return (x, lax.rem(zz, 2), lax.div(zz, 2), lax.rem(lax.div(p, 2), 4), lax.rem(p, 2))
+
+    barrier = pltpu.get_barrier_semaphore()
+
+    def greet(o, carry):
+        pl.semaphore_signal(barrier, inc=1, device_id=mate(o), device_id_type=MESH_ID)
+        return carry
+
+    lax.fori_loop(1, 32, greet, 0)
+    for o in range(1, 4):
+        pl.semaphore_signal(barrier, inc=1, device_id=dev(x_=m4(x + o)), device_id_type=MESH_ID)
 
     own_rows = pl.multiple_of(zl * R, R)
     own_cols = pl.multiple_of(v * U, U)
@@ -226,6 +210,7 @@
             comp[pl.ds(row, 2 * T), pl.ds(lane, U)]
         )
 
+    hidden_copy.wait()
     proj_copy.wait()
     for k in range(K):
         pre = nn(hidden[...], proj[k])
@@ -238,13 +223,31 @@
         own = at_ab(col, a, b, c)
         ag_send(col, 0, own, dev_ab(col, m4(a + 1), b))
         ag_send(col, 1, own, dev_ab(col, m4(a - 1), b))
-    info_copy.start()
     for col in range(2):
         a, b = pos(col)
         own = at_ab(col, a, b, c)
         second(col, 0, own)
         across(0, own)
 
+    mix_logits = nt(mix_t[...], hidden[...])
+    info2[zl, 0:4] = lse_t[...]
+    info2[zl, 4:8] = mix_logits - jnp.log(jnp.sum(jnp.exp(mix_logits), axis=0, keepdims=True))
+    info2[zl, 8:9] = scale[...]
+    info2[zl, 9:10] = target[...].astype(F32)
+    info2[zl, 10:16] = jnp.zeros((6, T), F32)
+
+    def row_columns(g):
+        cols = jnp.transpose(jnp.concatenate([info2[g], jnp.zeros((112, T), F32)], axis=0))
+        local = cols[:, 9:10] - (v * VL + zl * VH).astype(F32)
+        for k in range(K):
+            rows = pl.ds(pl.multiple_of(g * R + k * T, T), T)
+            lsec[rows, :] = jnp.broadcast_to(cols[:, k : k + 1], (T, 128))
+            tgtc[rows, :] = jnp.broadcast_to(local, (T, 128))
+
+    row_columns(zl)
+    info_copy = rc(info2.at[zl], info2.at[zl], sem_i.at[0], sem_i.at[1], partner_z)
+    info_copy.start()
+
     def hs_copy(i):
         p = m4(x + (0, 1, -1, 2)[i])
         return rc(
@@ -255,76 +258,106 @@
         hs_copy(i).start()
     hs[0] = hidden[:, pl.ds(pl.multiple_of(x * 512, 512), 512)]
 
-    def pick(n, carry):
-        rows = pl.ds(pl.multiple_of(n * 512, 512), 512)
-        acc = jnp.zeros((2 * T, 512), F32)
-        for q in range(4):
-            lane = lax.broadcasted_iota(jnp.int32, (T, 512), 1).astype(F32) + float(q * 512)
-            hot = jnp.concatenate(
-                [
-                    (lane == tgtc[pl.ds(g * R, T), :][:, 0:1]).astype(F32).astype(BF16)
-                    for g in range(2)
-                ],
-                axis=0,
-            )
-            acc = acc + nt(hot, w[rows, pl.ds(q * 512, 512)])
-        wt[:, rows] = acc.astype(BF16)
-        return carry
+    def pick(g):
+        def step(n, carry):
+            rows = pl.ds(pl.multiple_of(n * 512, 512), 512)
+            acc = jnp.zeros((T, 512), F32)
+            for q in range(4):
+                lane = lax.broadcasted_iota(jnp.int32, (T, 512), 1).astype(F32) + float(q * 512)
+                tgt = tgtc[pl.ds(pl.multiple_of(g * R, R), T), :][:, 0:1]
+                hot = (lane == tgt).astype(F32).astype(BF16)
+                acc = acc + nt(hot, w[rows, pl.ds(q * 512, 512)])
+            wt[pl.ds(pl.multiple_of(g * T, T), T), rows] = acc.astype(BF16)
+            return carry
+
+        lax.fori_loop(0, 4, step, 0)
+
+    w_copy.wait()
+    pick(zl)
 
     for col in range(2):
         a, b = pos(col)
         prev, nxt = m4(a - 1), m4(a + 1)
         ag_wait(col, 0, at_ab(col, prev, b, c))
         ag_send(col, 2, at_ab(col, prev, b, c, 0, T), dev_ab(col, nxt, b))
-        second(col, 1, at_ab(col, prev, b, c))
-        across(1, at_ab(col, prev, b, c))
         ag_wait(col, 1, at_ab(col, nxt, b, c))
         ag_send(col, 2, at_ab(col, nxt, b, c, T, T), dev_ab(col, prev, b))
-        second(col, 2, at_ab(col, nxt, b, c))
-        across(2, at_ab(col, nxt, b, c))
-    info_in = rc(info2.at[1 - zl], info2.at[1 - zl], sem_i.at[0], sem_i.at[1], partner_z)
-    info_in.wait_recv()
-    row_columns(1 - zl)
-    for col in range(2):
-        a, b = pos(col)
-        far = m4(a + 2)
-        ag_wait(col, 2, at_ab(col, far, b, c))
-        second(col, 3, at_ab(col, far, b, c))
-        across(3, at_ab(col, far, b, c))
-    w_copy.wait()
-    lax.fori_loop(0, 4, pick, 0)
-    for i in range(4):
+    for i, step in ((1, -1), (2, 1)):
+        for col in range(2):
+            a, b = pos(col)
+            second(col, i, at_ab(col, m4(a + step), b, c))
+            across(i, at_ab(col, m4(a + step), b, c))
+
+    def near(i):
         for col in range(2):
             a, b = pos(col)
             a_ = m4(a + (0, -1, 1, 2)[i])
             prev, nxt = m4(b - 1), m4(b + 1)
             ag_wait(col, 3 + 3 * i, at_ab(col, a_, prev, c))
             ag_send(col, 3 + 3 * i + 2, at_ab(col, a_, prev, c, 0, T), dev_ab(col, a, nxt))
-            across(i, at_ab(col, a_, prev, c))
             ag_wait(col, 3 + 3 * i + 1, at_ab(col, a_, nxt, c))
             ag_send(col, 3 + 3 * i + 2, at_ab(col, a_, nxt, c, T, T), dev_ab(col, a, prev))
+            across(i, at_ab(col, a_, prev, c))
             across(i, at_ab(col, a_, nxt, c))
-            for b_ in (b, prev, nxt):
-                flip(col, a_, b_, c)
-    for i in range(4):
+
+    def flip_near(i):
         for col in range(2):
             a, b = pos(col)
             a_ = m4(a + (0, -1, 1, 2)[i])
-            far = m4(b + 2)
-            ag_wait(col, 3 + 3 * i + 2, at_ab(col, a_, far, c))
-            across(i, at_ab(col, a_, far, c))
-            flip(col, a_, far, c)
-    for i in range(4):
-        ag_wait(None, i, comp.at[pl.ds(0, T), :])
+            for step in (0, -1, 1):
+                flip(col, a_, m4(b + step), c)
+
+    def far(i):
         for col in range(2):
             a, b = pos(col)
             a_ = m4(a + (0, -1, 1, 2)[i])
+            b_ = m4(b + 2)
+            ag_wait(col, 3 + 3 * i + 2, at_ab(col, a_, b_, c))
+            across(i, at_ab(col, a_, b_, c))
+            flip(col, a_, b_, c)
+
+    def partner_wait(i):
+        ag_wait(None, i, comp.at[pl.ds(0, T), :])
+
+    def flip_partner(i):
+        for col in range(2):
+            a, b = pos(col)
+            a_ = m4(a + (0, -1, 1, 2)[i])
 
             def flip_step(b_, carry):
                 flip(col, a_, b_, 1 - c)
                 return carry
 
             lax.fori_loop(0, 4, flip_step, 0)
+
+    near(0)
+    info_in = rc(info2.at[1 - zl], info2.at[1 - zl], sem_i.at[0], sem_i.at[1], partner_z)
+    info_in.wait_recv()
+    row_columns(1 - zl)
+    pick(1 - zl)
+    for col in range(2):
+        a, b = pos(col)
+        two = m4(a + 2)
+        ag_wait(col, 2, at_ab(col, two, b, c))
+        second(col, 3, at_ab(col, two, b, c))
+        across(3, at_ab(col, two, b, c))
+    near(1)
+    near(2)
+    for i in range(3):
+        flip_near(i)
+    far(0)
+    near(3)
+    partner_wait(0)
+    flip_partner(0)
+    far(1)
+    far(2)
+    flip_near(3)
+    partner_wait(1)
+    flip_partner(1)
+    partner_wait(2)
+    flip_partner(2)
+    far(3)
+    partner_wait(3)
 
     lane_t = lax.broadcasted_iota(jnp.int32, (T, 128), 1)
     acc = jnp.zeros((T, 128), F32)
@@ -369,6 +402,7 @@
         return carry
 
     lax.fori_loop(0, 4, hold, 0)
+    flip_partner(3)
 
     tl_all = rc(tl.at[pl.ds(1, 31)], tl.at[pl.ds(1, 31)], tl_s, tl_r, partner_c)
     tl_all.wait_recv()
@@ -383,20 +417,18 @@
         resp = weights / jnp.sum(weights, axis=0, keepdims=True)
         coef_rows.append(scale_g * resp)
         gml_rows.append(-scale_g * (resp - jnp.exp(lm_g)))
-    table = jnp.concatenate(coef_rows + gml_rows + [jnp.zeros((112, 128), F32)], axis=0)
+    table = jnp.concatenate(coef_rows + [jnp.zeros((120, 128), F32)], axis=0)
     cols = jnp.transpose(table)
     for g in range(2):
         for k in range(K):
             coefc[pl.ds(g * R + k * T, T), :] = jnp.broadcast_to(
                 cols[:, g * K + k : g * K + k + 1], (T, 128)
             )
-    gml = jnp.zeros((T, 128), F32)
-    for k in range(K):
-        mine = jnp.where(zl == 0, cols[:, 8 + k : 9 + k], cols[:, 12 + k : 13 + k])
-        high = mine.astype(BF16).astype(F32)
-        gml = jnp.where(lane_t == k, high, gml)
-        gml = jnp.where(lane_t == K + k, mine - high, gml)
-    gpx[4] = gml.astype(BF16)
+    mine = jnp.where(zl == 0, gml_rows[0], gml_rows[1])
+    high = mine.astype(BF16).astype(F32)
+    gmla[0] = jnp.concatenate([high, mine - high, jnp.zeros((8, T), F32)], axis=0).astype(BF16)
+    for i in range(1, 4):
+        rc(gmla.at[0], gmla.at[i], gm_s, gm_r, dev(x_=m4(x + (0, 1, -1, 2)[i]))).start()
 
     def ring(piece, me, right, left, r1, rf, ss, r1_sem, rf_sem, r1_all, rf_all):
         two, one, back = m4(me + 2), m4(me + 1), m4(me - 1)
@@ -445,16 +477,17 @@
             rfx.at[cc],
         )
 
-    def grad_out(p):
+    def grad_out(p, tiles, send=True):
         cols = pl.ds(p * W2, W2)
         order = ((2, 0), (2, 1), (1, 1), (-1, 0), (1, 0), (-1, 1), (0, 0), (0, 1))
-        for i, (step, h) in enumerate(order):
+        for i in tiles:
+            step, h = order[i]
             t = m4(x + step)
             rows = pl.ds(pl.multiple_of(t * 512 + h * 256, 256), 256)
             res = nn(comp_t[rows, :], gl[:, cols]).astype(BF16)
             for e in range(2):
                 part[2 * p + e, t * 2 + h] = res[:, e * C : (e + 1) * C]
-            if i < 4:
+            if send and i < 4:
                 for e in range(2):
                     x_ring(2 * p + e)[0](((0, 2, 1, 3)[i],))
 
@@ -481,84 +514,100 @@
 
         lax.fori_loop(0, 4, rows_of, 0)
 
-    def comp_grad(col):
+    def comp_grad(bat):
         def tile(i, carry):
             g, h, j = lax.div(i, 4), lax.rem(lax.div(i, 2), 2), lax.rem(i, 2)
-            rows = pl.ds(pl.multiple_of(g * R + col * 2 * T, 2 * T), 2 * T)
+            rows = pl.ds(pl.multiple_of(g * R + bat * 2 * T, 2 * T), 2 * T)
             units = pl.ds(pl.multiple_of((h * 2 + j) * 512, 512), 512)
             res = nt(gl[rows, :], w[units, :])
             z_ = h * 2 + g
             for jj in range(4):
                 y_ = j * 2 + jj // 2
                 val = res[:, jj * 128 : (jj + 1) * 128].astype(BF16)
-                if col == 0:
-                    gcb[jj % 2, col, z_, y_] = val
-                else:
-                    gcb[jj % 2, col, y_, z_] = val
+                gcb[jj % 2, 2 * bat, z_, y_] = val[0:T]
+                gcb[jj % 2, 2 * bat + 1, y_, z_] = val[T : 2 * T]
             return carry
 
-        lax.fori_loop(0, 8, tile, 0)
-        swap = rc(gcb.at[1 - c, col], rd.at[col], d_s.at[col], d_r.at[col], partner_c)
+        lax.fori_loop(0, 6, tile, 0)
+        if bat == 1:
+            x_finish(0)
+        lax.fori_loop(6, 8, tile, 0)
+        two = pl.ds(2 * bat, 2)
+        swap = rc(gcb.at[1 - c, two], rd.at[two], d_s.at[bat], d_r.at[bat], partner_c)
         swap.start()
         return swap
 
-    def a_ring(col):
-        me = z if col == 0 else y
-        mk = (lambda p: dev(z_=p)) if col == 0 else (lambda p: dev(y_=p))
+    def a_ring(k):
+        me = z if k % 2 == 0 else y
+        mk = (lambda p: dev(z_=p)) if k % 2 == 0 else (lambda p: dev(y_=p))
         return ring(
-            lambda t, h: gcb.at[c, col, t, pl.ds(2 * h, 2)],
+            lambda t, h: gcb.at[c, k, t, pl.ds(2 * h, 2)],
             me,
             mk(m4(me + 1)),
             mk(m4(me - 1)),
-            lambda i: r1a.at[col, i],
-            lambda i, h: rfa.at[col, i, h],
+            lambda i: r1a.at[k, i],
+            lambda i, h: rfa.at[k, i, h],
             a_s,
-            a_r.at[2 * col],
-            a_r.at[2 * col + 1],
-            r1a.at[col],
-            rfa.at[col],
+            a_r.at[2 * k],
+            a_r.at[2 * k + 1],
+            r1a.at[k],
+            rfa.at[k],
         )
 
-    def b_ring(col):
-        first = z if col == 0 else y
-        me = y if col == 0 else z
-        mk = (lambda p: dev(y_=p)) if col == 0 else (lambda p: dev(z_=p))
-        return ring(
-            lambda t, h: gcb.at[c, col, first, t, pl.ds(h * T, T)],
-            me,
-            mk(m4(me + 1)),
-            mk(m4(me - 1)),
-            lambda i: r1b.at[col, i],
-            lambda i, h: rfb.at[col, i, h],
-            b_s,
-            b_r.at[2 * col],
-            b_r.at[2 * col + 1],
-            r1b.at[col],
-            rfb.at[col],
-        )
-
-    def merge(col, swap):
+    def b_copies(k):
+        first, me = (z, y) if k % 2 == 0 else (y, z)
+        mk = (lambda p: dev(y_=p)) if k % 2 == 0 else (lambda p: dev(z_=p))
+        return [
+            rc(gcb.at[c, k, first, t], rfb.at[k, o - 1], b_s, b_r.at[k], mk(t))
+            for o in range(1, 4)
+            for t in [m4(me + o)]
+        ]
+
+    def merge(bat, swap):
         swap.wait_recv()
 
         def add(i, carry):
             p, q = lax.div(i, 4), lax.rem(i, 4)
-            gcb[c, col, p, q] = (gcb[c, col, p, q].astype(F32) + rd[col, p, q].astype(F32)).astype(
-                BF16
-            )
+            for k in (2 * bat, 2 * bat + 1):
+                gcb[c, k, p, q] = (
+                    gcb[c, k, p, q].astype(F32) + rd[k, p, q].astype(F32)
+                ).astype(BF16)
             return carry
 
         lax.fori_loop(0, 16, add, 0)
-
-    def finish_a(col):
-        me = z if col == 0 else y
-        for h in range(2):
-            for e in range(2):
-                q = 2 * h + e
-                gcb[c, col, me, q] = (
-                    gcb[c, col, me, q].astype(F32)
-                    + rfa[col, 0, h, e].astype(F32)
-                    + rfa[col, 1, h, e].astype(F32)
-                ).astype(BF16)
+        for k in (2 * bat, 2 * bat + 1):
+            a_ring(k)[0]()
+
+    def forward_a(bat):
+        for k in (2 * bat, 2 * bat + 1):
+            a_ring(k)[1]()
+
+    def finish_a(bat):
+        for k in (2 * bat, 2 * bat + 1):
+            a_ring(k)[2]()
+            me = z if k % 2 == 0 else y
+            for h in range(2):
+                for e in range(2):
+                    q = 2 * h + e
+                    gcb[c, k, me, q] = (
+                        gcb[c, k, me, q].astype(F32)
+                        + rfa[k, 0, h, e].astype(F32)
+                        + rfa[k, 1, h, e].astype(F32)
+                    ).astype(BF16)
+            for cp in b_copies(k):
+                cp.start()
+
+    def finish_b(bat):
+        for k in (2 * bat, 2 * bat + 1):
+            rc(rfb.at[k], rfb.at[k], b_s, b_r.at[k], partner_c).wait_recv()
+            first, me = (z, y) if k % 2 == 0 else (y, z)
+            total = gcb[c, k, first, me].astype(F32)
+            for o in range(3):
+                total = total + rfb[k, o].astype(F32)
+            cf = comp[
+                pl.ds(pl.multiple_of(own_rows + k * T, T), T), pl.ds(own_cols, U)
+            ].astype(F32)
+            gpx[k] = (total * (1.0 - cf * cf)).astype(BF16)
 
     def x_finish(cc):
         x_ring(cc)[2]()
@@ -579,56 +628,36 @@
             pltpu.make_async_copy(part.at[cc, x * 2 + zl], dst, zx_l),
         )
 
-    def finish_b(col):
-        first = z if col == 0 else y
-        me = y if col == 0 else z
-        b_ring(col)[2]()
-        for h in range(2):
-            total = (
-                gcb[c, col, first, me, pl.ds(h * T, T)].astype(F32)
-                + rfb[col, 0, h].astype(F32)
-                + rfb[col, 1, h].astype(F32)
-            )
-            k = 2 * col + h
-            cf = comp[
-                pl.ds(pl.multiple_of(own_rows + k * T, T), T), pl.ds(own_cols, U)
-            ].astype(F32)
-            gpx[k] = (total * (1.0 - cf * cf)).astype(BF16)
-
-    grad_out(0)
+    first_half, second_half, every = range(4), range(4, 8), range(8)
+    grad_out(0, every)
     grad_logits(1)
-    grad_out(1)
+    grad_out(1, every)
     x_ring(0)[1]()
     grad_logits(2)
     grad_logits(3)
     x_ring(1)[1]()
     swap0 = comp_grad(0)
-    grad_out(2)
+    x_ring(2)[1]()
+    grad_out(2, first_half)
     merge(0, swap0)
-    a_ring(0)[0]()
-    x_ring(2)[1]()
     swap1 = comp_grad(1)
-    a_ring(0)[1]()
+    forward_a(0)
     x_ring(3)[1]()
-    grad_out(3)
+    x_finish(1)
+    grad_out(2, second_half)
     merge(1, swap1)
-    a_ring(1)[0]()
-    x_finish(0)
-    a_ring(0)[2]()
     finish_a(0)
-    b_ring(0)[0]()
-    a_ring(1)[1]()
     hs_all = rc(hs.at[pl.ds(1, 3)], hs.at[pl.ds(1, 3)], hs_s, hs_r, partner_c)
     hs_all.wait_recv()
     for i in range(4):
         hst[:, pl.ds(i * T, T)] = jnp.transpose(hs[i])
-    b_ring(0)[1]()
-    x_finish(1)
-    a_ring(1)[2]()
+    grad_out(3, first_half, False)
+    forward_a(1)
+    x_finish(2)
+    grad_out(3, second_half, False)
+    x_ring(4)[1]()
+    finish_b(0)
     finish_a(1)
-    b_ring(1)[0]()
-    finish_b(0)
-    b_ring(1)[1]()
     finish_b(1)
 
     def slot(i, r0=0, n=T):
@@ -642,7 +671,7 @@
     )
     g_copies[0].start()
     g_copies[1].start()
-    x_ring(4)[1]()
+    x_ring(6)[0]()
 
     def h_copy(o):
         p = lax.rem(v + o, 16)
@@ -665,15 +694,48 @@
     lax.fori_loop(1, 16, h_step, 0)
     hrecv[0] = h_tile(0).astype(BF16)
     gpall[:, pl.ds(0, T)] = gpx[...]
+    x_finish(3)
+    x_finish(4)
+    g_copies[0].wait_recv()
+    g_copies[2].start()
+    g_copies[1].wait_recv()
+    g_copies[3].start()
     x_ring(5)[1]()
-    x_finish(2)
-    x_finish(3)
+    x_ring(7)[0]()
+
+    rc(slot(3), slot(3), g_s, g_r.at[2], x_right).wait_recv()
+
+    def product(half, k):
+        return nn(hst[pl.ds(pl.multiple_of(half * 256, 256), 256), :], gpall[k])
+
+    def mix_product(half):
+        rows = pl.ds(pl.multiple_of(half * 256, 256), 256)
+        res = nt(gmla[0], hst[rows, pl.ds(0, T)])
+        for i in range(1, 4):
+            res = res + nt(gmla[i], hst[rows, pl.ds(i * T, T)])
+        return res[0:4] + res[4:8]
+
+    for k in range(K):
+        prods[k] = product(1 - zl, k).astype(BF16)
+    gm_all = rc(gmla.at[pl.ds(1, 3)], gmla.at[pl.ds(1, 3)], gm_s, gm_r, partner_c)
+    gm_all.wait_recv()
+    gms[...] = mix_product(1 - zl)
+    p_copies = (
+        rc(prods, prodr, p_s.at[0], p_r.at[0], partner_z),
+        rc(gms, gmr, p_s.at[1], p_r.at[1], partner_z),
+    )
+    for cp in p_copies:
+        cp.start()
+    x_ring(6)[1]()
+    x_finish(5)
+    x_ring(7)[1]()
+    x_finish(6)
     h_all = rc(hts.at[pl.ds(1, 15)], hrecv.at[pl.ds(1, 15)], h_s, h_r, partner_c)
     h_all.wait_recv()
     mw = jnp.concatenate(
-        [mix_t[:, pl.ds(own_cols, U)].astype(F32)] * 2 + [jnp.zeros((120, U), F32)], axis=0
+        [mix_t[:, pl.ds(own_cols, U)].astype(F32)] * 2 + [jnp.zeros((8, U), F32)], axis=0
     ).astype(BF16)
-    gh = nn(gpx[4], mw)
+    gh = lax.dot_general(gmla[0], mw, (((0,), (0,)), ((), ())), preferred_element_type=F32)
     for o in range(16):
         gh = gh + hrecv[o].astype(F32)
     gh_v[...] = gh.astype(BF16)
@@ -683,39 +745,6 @@
         pltpu.make_async_copy(gm_v, gm_out, sem_o.at[2]),
     )
     out_copies[0].start()
-    x_ring(6)[1]()
-    g_copies[0].wait_recv()
-    g_copies[2].start()
-    g_copies[1].wait_recv()
-    g_copies[3].start()
-    x_ring(7)[1]()
-    x_finish(4)
-    x_finish(5)
-
-    rc(slot(3), slot(3), g_s, g_r.at[2], x_right).wait_recv()
-
-    def product(half, k):
-        return nn(hst[pl.ds(pl.multiple_of(half * 256, 256), 256), :], gpall[k])
-
-    def mix_product(half):
-        res = lax.dot_general(
-            gpall[4],
-            hst[pl.ds(pl.multiple_of(half * 256, 256), 256), :],
-            (((0,), (1,)), ((), ())),
-            preferred_element_type=F32,
-        )
-        return res[0:4] + res[4:8]
-
-    for k in range(K):
-        prods[k] = product(1 - zl, k).astype(BF16)
-    gms[...] = mix_product(1 - zl)
-    p_copies = (
-        rc(prods, prodr, p_s.at[0], p_r.at[0], partner_z),
-        rc(gms, gmr, p_s.at[1], p_r.at[1], partner_z),
-    )
-    for cp in p_copies:
-        cp.start()
-    x_finish(6)
     x_finish(7)
     for cp in p_copies:
         cp.wait_recv()
@@ -725,14 +754,14 @@
     out_copies[1].start()
     out_copies[2].start()
 
-    for cp in (info_copy, swap0, swap1, *p_copies, tl_all, hs_all, h_all):
+    for cp in (info_copy, swap0, swap1, *p_copies, tl_all, hs_all, h_all, gm_all):
         cp.wait_send()
     for ref, sem in (
         (comp.at[pl.ds(0, 992), :], ag_s),
         (part.at[pl.ds(0, 6)], x_s),
         (part.at[0], zx_s),
-        (gcb.at[0, :, pl.ds(0, 3)], a_s),
-        (gcb.at[0, 0, pl.ds(0, 3), pl.ds(0, 2)], b_s),
+        (gcb.at[0, pl.ds(0, 3)], a_s),
+        (gcb.at[0, 0, pl.ds(0, 3)], b_s),
         (gpall.at[:, pl.ds(0, 3 * T)], g_s),
     ):
         rc(ref, ref, sem, zx_r, partner_z).wait_send()
@@ -784,17 +813,17 @@
             pltpu.VMEM((NC, 8, 256, C), BF16),
             pltpu.VMEM((NC, 2, 256, C), BF16),
             pltpu.VMEM((NC, 2, 2, 256, C), BF16),
-            pltpu.VMEM((2, 2, 4, 4, 2 * T, U), BF16),
-            pltpu.VMEM((2, 4, 4, 2 * T, U), BF16),
-            pltpu.VMEM((2, 2, 2, 2 * T, U), BF16),
-            pltpu.VMEM((2, 2, 2, 2, 2 * T, U), BF16),
-            pltpu.VMEM((2, 2, T, U), BF16),
-            pltpu.VMEM((2, 2, 2, T, U), BF16),
+            pltpu.VMEM((2, 4, 4, 4, T, U), BF16),
+            pltpu.VMEM((4, 4, 4, T, U), BF16),
+            pltpu.VMEM((4, 2, 2, T, U), BF16),
+            pltpu.VMEM((4, 2, 2, 2, T, U), BF16),
+            pltpu.VMEM((4, 3, T, U), BF16),
             pltpu.VMEM((2 * T, D), BF16),
             pltpu.VMEM((4, T, 512), BF16),
             pltpu.VMEM((512, 4 * T), BF16),
-            pltpu.VMEM((5, T, U), BF16),
-            pltpu.VMEM((5, 4 * T, U), BF16),
+            pltpu.VMEM((K, T, U), BF16),
+            pltpu.VMEM((K, 4 * T, U), BF16),
+            pltpu.VMEM((4, 16, T), BF16),
             pltpu.VMEM((K, 256, U), BF16),
             pltpu.VMEM((K, 256, U), BF16),
             pltpu.VMEM((K, 256), F32),
@@ -829,13 +858,15 @@
             dma((2,)),
             dma((2,)),
             dma,
+            dma((8,)),
+            dma,
             dma((4,)),
             dma,
-            dma((4,)),
-            dma,
             dma,
             dma,
             dma((3,)),
+            dma,
+            dma,
         ],
         compiler_params=pltpu.CompilerParams(
             collective_id=0, has_side_effects=True, vmem_limit_bytes=67043328

time: 126 us -> 117 us (0.929)
  Pallas kernels: 124 us -> 115 us
    pallas_call x1, Pallas kernels: 121 us -> 113 us  [shards(): pl.pallas_call(kernel, out_shape=outs, in_specs=[vm, vm, vm, vm, hbm, hbm...]
where the time goes in v3:
time: 117 us; the launch traced here: 116 us
  Pallas kernels  115 us (98%)
    pallas_call x1, Pallas kernels, shards(): pl.pallas_call(kernel, out_shape=outs, in_specs=[vm, vm, vm, vm, hbm, hbm...  113 us
    pallas_call x1, Pallas kernels, shards(): pl.pallas_call(place, out_shape=outs, in_specs=[hbm] * 4, out_specs=(hbm,...  2.57 us

profile of v3, /device:TPU:1, one launch (start us, length us, event | category | flops | bytes accessed | tf_op | source)
XLA Modules:
  0.0 116.2 jit_solution(15586990654188200250)
XLA Ops:
  0.6 112.8 %shard_map.102 = (bf16[128,128]{1,0:T(8,128)(2,1)}, f32[4,256]{1,0:T(4,128)}, bf16[4,256,128]{2,1,0:T(8,128)(2,1)}, bf16[256,4096]{1,0:T(8,128)(2,1)}) custom-call(bf16[4,2048]{1,0:T(4,128)(2,1)} %bitcast.5, f32[4,128]{1,0:T(4,128)} %bitcast.6, f32[1,128]{1,0:T(1,128)} %bitcast.7, s32[1,128]{1,0:T(1,128)} %bitcast.8, bf16[128,2048]{1,0:T(8,128)(2,1)} %hidden_hbm.1, ...), custom_call_target="tpu_custom_call" | custom-call | tf_op jit(solution)/shard_map/pallas_call | solution.py:801
  113.5 2.6 %shard_map.103 = (bf16[128,128]{1,0:T(8,128)(2,1)}, f32[4,256]{1,0:T(4,128)}, bf16[4,256,128]{2,1,0:T(8,128)(2,1)}, bf16[256,4096]{1,0:T(8,128)(2,1)}) custom-call(bf16[128,128]{1,0:T(8,128)(2,1)} %get-tuple-element.12.gh, f32[4,256]{1,0:T(4,128)} %get-tuple-element.13.gm, bf16[4,256,128]{2,1,0:T(8,128)(2,1)} %get-tuple-element.14.gp, ...), custom_call_target="tpu_custom_call" | custom-call | tf_op jit(solution)/shard_map/pallas_call | solution.py:883

commit v4 on v3

--- a/solution.py
+++ b/solution.py
@@ -78,6 +78,7 @@
     coefc,
     tgtc,
     tl,
+    tacc,
     pbuf,
     gh_v,
     gm_v,
@@ -167,13 +168,11 @@
     for o in range(1, 4):
         pl.semaphore_signal(barrier, inc=1, device_id=dev(x_=m4(x + o)), device_id_type=MESH_ID)
 
-    own_rows = pl.multiple_of(zl * R, R)
     own_cols = pl.multiple_of(v * U, U)
 
     def blk(col, z_, y_, c_, r0=0, n=2 * T):
-        row = lax.rem(z_, 2) * R + col * 2 * T + r0
-        lane = (lax.div(z_, 2) * 8 + y_ * 2 + c_) * U
-        return comp.at[pl.ds(pl.multiple_of(row, T), n), pl.ds(pl.multiple_of(lane, U), U)]
+        block = lax.rem(z_, 2) * 16 + lax.div(z_, 2) * 8 + y_ * 2 + c_
+        return comp.at[block, pl.ds(col * 2 * T + r0, n)]
 
     def pos(col):
         return (y, z) if col == 0 else (z, y)
@@ -205,29 +204,32 @@
     def flip(col, a_, b_, c_):
         z_, y_ = (b_, a_) if col == 0 else (a_, b_)
         row = pl.multiple_of(lax.rem(z_, 2) * R + col * 2 * T, 2 * T)
-        lane = pl.multiple_of((lax.div(z_, 2) * 8 + y_ * 2 + c_) * U, U)
-        comp_t[pl.ds(lane, U), pl.ds(row, 2 * T)] = jnp.transpose(
-            comp[pl.ds(row, 2 * T), pl.ds(lane, U)]
+        unit = lax.div(z_, 2) * 8 + y_ * 2 + c_
+        comp_t[pl.ds(pl.multiple_of(unit * U, U), U), pl.ds(row, 2 * T)] = jnp.transpose(
+            comp[lax.rem(z_, 2) * 16 + unit, pl.ds(col * 2 * T, 2 * T)]
         )
+
+    def gauge(col, a_, b_, c_):
+        z_, y_ = (b_, a_) if col == 0 else (a_, b_)
+        g = lax.rem(z_, 2)
+        unit = lax.div(z_, 2) * 8 + y_ * 2 + c_
+        weight = wt[
+            pl.ds(pl.multiple_of(g * T, T), T), pl.ds(pl.multiple_of(unit * U, U), U)
+        ].astype(F32)
+        for k in (2 * col, 2 * col + 1):
+            tacc[g * K + k] += comp[g * 16 + unit, pl.ds(k * T, T)].astype(F32) * weight
 
     hidden_copy.wait()
     proj_copy.wait()
     for k in range(K):
         pre = nn(hidden[...], proj[k])
-        comp[pl.ds(pl.multiple_of(own_rows + k * T, T), T), pl.ds(own_cols, U)] = jnp.tanh(
-            pre
-        ).astype(BF16)
+        comp[zl * 16 + v, pl.ds(k * T, T)] = jnp.tanh(pre).astype(BF16)
     pl.semaphore_wait(barrier, 34)
     for col in range(2):
         a, b = pos(col)
         own = at_ab(col, a, b, c)
         ag_send(col, 0, own, dev_ab(col, m4(a + 1), b))
         ag_send(col, 1, own, dev_ab(col, m4(a - 1), b))
-    for col in range(2):
-        a, b = pos(col)
-        own = at_ab(col, a, b, c)
-        second(col, 0, own)
-        across(0, own)
 
     mix_logits = nt(mix_t[...], hidden[...])
     info2[zl, 0:4] = lse_t[...]
@@ -248,6 +250,12 @@
     info_copy = rc(info2.at[zl], info2.at[zl], sem_i.at[0], sem_i.at[1], partner_z)
     info_copy.start()
 
+    for col in range(2):
+        a, b = pos(col)
+        own = at_ab(col, a, b, c)
+        second(col, 0, own)
+        across(0, own)
+
     def hs_copy(i):
         p = m4(x + (0, 1, -1, 2)[i])
         return rc(
@@ -258,22 +266,21 @@
         hs_copy(i).start()
     hs[0] = hidden[:, pl.ds(pl.multiple_of(x * 512, 512), 512)]
 
-    def pick(g):
-        def step(n, carry):
-            rows = pl.ds(pl.multiple_of(n * 512, 512), 512)
-            acc = jnp.zeros((T, 512), F32)
-            for q in range(4):
-                lane = lax.broadcasted_iota(jnp.int32, (T, 512), 1).astype(F32) + float(q * 512)
-                tgt = tgtc[pl.ds(pl.multiple_of(g * R, R), T), :][:, 0:1]
-                hot = (lane == tgt).astype(F32).astype(BF16)
-                acc = acc + nt(hot, w[rows, pl.ds(q * 512, 512)])
-            wt[pl.ds(pl.multiple_of(g * T, T), T), rows] = acc.astype(BF16)
-            return carry
-
-        lax.fori_loop(0, 4, step, 0)
-
-    w_copy.wait()
-    pick(zl)
+    def pick(n, carry):
+        rows = pl.ds(pl.multiple_of(n * 512, 512), 512)
+        acc = jnp.zeros((2 * T, 512), F32)
+        for q in range(4):
+            lane = lax.broadcasted_iota(jnp.int32, (T, 512), 1).astype(F32) + float(q * 512)
+            hot = jnp.concatenate(
+                [
+                    (lane == tgtc[pl.ds(g * R, T), :][:, 0:1]).astype(F32).astype(BF16)
+                    for g in range(2)
+                ],
+                axis=0,
+            )
+            acc = acc + nt(hot, w[rows, pl.ds(q * 512, 512)])
+        wt[:, rows] = acc.astype(BF16)
+        return carry
 
     for col in range(2):
         a, b = pos(col)
@@ -306,6 +313,7 @@
             a_ = m4(a + (0, -1, 1, 2)[i])
             for step in (0, -1, 1):
                 flip(col, a_, m4(b + step), c)
+                gauge(col, a_, m4(b + step), c)
 
     def far(i):
         for col in range(2):
@@ -315,32 +323,40 @@
             ag_wait(col, 3 + 3 * i + 2, at_ab(col, a_, b_, c))
             across(i, at_ab(col, a_, b_, c))
             flip(col, a_, b_, c)
+            gauge(col, a_, b_, c)
 
     def partner_wait(i):
-        ag_wait(None, i, comp.at[pl.ds(0, T), :])
-
-    def flip_partner(i):
+        ag_wait(None, i, comp.at[pl.ds(0, 4)])
+
+    def on_partner(i, act):
         for col in range(2):
             a, b = pos(col)
             a_ = m4(a + (0, -1, 1, 2)[i])
 
-            def flip_step(b_, carry):
-                flip(col, a_, b_, 1 - c)
+            def step(b_, carry):
+                act(col, a_, b_, 1 - c)
                 return carry
 
-            lax.fori_loop(0, 4, flip_step, 0)
-
+            lax.fori_loop(0, 4, step, 0)
+
+    def both(*where):
+        flip(*where)
+        gauge(*where)
+
+    tacc[...] = jnp.zeros_like(tacc)
     near(0)
     info_in = rc(info2.at[1 - zl], info2.at[1 - zl], sem_i.at[0], sem_i.at[1], partner_z)
     info_in.wait_recv()
     row_columns(1 - zl)
-    pick(1 - zl)
+    w_copy.wait()
+    lax.fori_loop(0, 2, pick, 0)
     for col in range(2):
         a, b = pos(col)
         two = m4(a + 2)
         ag_wait(col, 2, at_ab(col, two, b, c))
         second(col, 3, at_ab(col, two, b, c))
         across(3, at_ab(col, two, b, c))
+    lax.fori_loop(2, 4, pick, 0)
     near(1)
     near(2)
     for i in range(3):
@@ -348,29 +364,23 @@
     far(0)
     near(3)
     partner_wait(0)
-    flip_partner(0)
+    on_partner(0, both)
     far(1)
     far(2)
     flip_near(3)
     partner_wait(1)
-    flip_partner(1)
+    on_partner(1, both)
     partner_wait(2)
-    flip_partner(2)
+    on_partner(2, both)
     far(3)
     partner_wait(3)
+    on_partner(3, gauge)
 
     lane_t = lax.broadcasted_iota(jnp.int32, (T, 128), 1)
     acc = jnp.zeros((T, 128), F32)
     for g in range(2):
         for k in range(K):
-            s = jnp.zeros((T, 128), F32)
-            for q in range(4):
-                prod = comp[pl.ds(g * R + k * T, T), pl.ds(q * 512, 512)].astype(F32) * wt[
-                    pl.ds(g * T, T), pl.ds(q * 512, 512)
-                ].astype(F32)
-                for e in range(4):
-                    s = s + prod[:, e * 128 : (e + 1) * 128]
-            acc = jnp.where(lane_t == g * K + k, jnp.sum(s, axis=1, keepdims=True), acc)
+            acc = jnp.where(lane_t == g * K + k, jnp.sum(tacc[g * K + k], axis=1, keepdims=True), acc)
     tl[0] = jnp.transpose(acc)[0:8]
 
     def tl_copy(o):
@@ -386,7 +396,9 @@
 
     def block_logits(p, m, put):
         rows = pl.ds(pl.multiple_of(m * 2 * T, 2 * T), 2 * T)
-        logit = nn(comp[rows, :], w[:, pl.ds(pl.multiple_of(p * W2, W2), W2)])
+        g, part_rows = lax.div(m, 2), pl.ds(pl.multiple_of(lax.rem(m, 2) * 2 * T, 2 * T), 2 * T)
+        vectors = jnp.concatenate([comp[g * 16 + u, part_rows] for u in range(16)], axis=1)
+        logit = nn(vectors, w[:, pl.ds(pl.multiple_of(p * W2, W2), W2)])
         shift = jnp.asarray(p * W2, F32)
         lse_m, tgt_m = lsec[rows, :], tgtc[rows, :] - shift
         for e in range(W2 // 128):
@@ -402,7 +414,7 @@
         return carry
 
     lax.fori_loop(0, 4, hold, 0)
-    flip_partner(3)
+    on_partner(3, flip)
 
     tl_all = rc(tl.at[pl.ds(1, 31)], tl.at[pl.ds(1, 31)], tl_s, tl_r, partner_c)
     tl_all.wait_recv()
@@ -462,19 +474,21 @@
 
     x_right, x_left = dev(x_=m4(x + 1)), dev(x_=m4(x - 1))
 
-    def x_ring(cc):
+    def x_ring(cc, e=None):
+        lanes = pl.ds(0, C) if e is None else pl.ds(e * 128, 128)
+        sem = 2 * cc if e is None else 2 * NC + 2 * (2 * (cc - 6) + e)
         return ring(
-            lambda t, h: part.at[cc, t * 2 + h],
+            lambda t, h: part.at[cc, t * 2 + h, :, lanes],
             x,
             x_right,
             x_left,
-            lambda i: r1x.at[cc, i],
-            lambda i, h: rfx.at[cc, i, h],
+            lambda i: r1x.at[cc, i, :, lanes],
+            lambda i, h: rfx.at[cc, i, h, :, lanes],
             x_s,
-            x_r.at[2 * cc],
-            x_r.at[2 * cc + 1],
-            r1x.at[cc],
-            rfx.at[cc],
+            x_r.at[sem],
+            x_r.at[sem + 1],
+            r1x.at[cc, :, :, lanes],
+            rfx.at[cc, :, :, :, lanes],
         )
 
     def grad_out(p, tiles, send=True):
@@ -528,10 +542,7 @@
                 gcb[jj % 2, 2 * bat + 1, y_, z_] = val[T : 2 * T]
             return carry
 
-        lax.fori_loop(0, 6, tile, 0)
-        if bat == 1:
-            x_finish(0)
-        lax.fori_loop(6, 8, tile, 0)
+        lax.fori_loop(0, 8, tile, 0)
         two = pl.ds(2 * bat, 2)
         swap = rc(gcb.at[1 - c, two], rd.at[two], d_s.at[bat], d_r.at[bat], partner_c)
         swap.start()
@@ -604,29 +615,25 @@
             total = gcb[c, k, first, me].astype(F32)
             for o in range(3):
                 total = total + rfb[k, o].astype(F32)
-            cf = comp[
-                pl.ds(pl.multiple_of(own_rows + k * T, T), T), pl.ds(own_cols, U)
-            ].astype(F32)
+            cf = comp[zl * 16 + v, pl.ds(k * T, T)].astype(F32)
             gpx[k] = (total * (1.0 - cf * cf)).astype(BF16)
 
-    def x_finish(cc):
-        x_ring(cc)[2]()
+    def x_finish(cc, e=None):
+        lanes = pl.ds(0, C) if e is None else pl.ds(e * 128, 128)
+        x_ring(cc, e)[2]()
         for h in range(2):
-            part[cc, x * 2 + h] = (
-                part[cc, x * 2 + h].astype(F32)
-                + rfx[cc, 0, h].astype(F32)
-                + rfx[cc, 1, h].astype(F32)
+            part[cc, x * 2 + h, :, lanes] = (
+                part[cc, x * 2 + h, :, lanes].astype(F32)
+                + rfx[cc, 0, h, :, lanes].astype(F32)
+                + rfx[cc, 1, h, :, lanes].astype(F32)
             ).astype(BF16)
-        for cp in z_copies(cc):
-            cp.start()
-
-    def z_copies(cc):
-        cols = pl.ds(pl.multiple_of(zl * VH + cc * C, C), C)
+        if e is None:
+            cols = pl.ds(pl.multiple_of(zl * VH + cc * C, C), C)
+        else:
+            cols = pl.ds(pl.multiple_of(zl * VH + cc * C + e * 128, 128), 128)
         dst = go_out.at[:, cols]
-        return (
-            rc(part.at[cc, x * 2 + 1 - zl], dst, zx_s, zx_r, partner_z),
-            pltpu.make_async_copy(part.at[cc, x * 2 + zl], dst, zx_l),
-        )
+        rc(part.at[cc, x * 2 + 1 - zl, :, lanes], dst, zx_s, zx_r, partner_z).start()
+        pltpu.make_async_copy(part.at[cc, x * 2 + zl, :, lanes], dst, zx_l).start()
 
     first_half, second_half, every = range(4), range(4, 8), range(8)
     grad_out(0, every)
@@ -643,7 +650,6 @@
     swap1 = comp_grad(1)
     forward_a(0)
     x_ring(3)[1]()
-    x_finish(1)
     grad_out(2, second_half)
     merge(1, swap1)
     finish_a(0)
@@ -653,11 +659,13 @@
         hst[:, pl.ds(i * T, T)] = jnp.transpose(hs[i])
     grad_out(3, first_half, False)
     forward_a(1)
-    x_finish(2)
     grad_out(3, second_half, False)
     x_ring(4)[1]()
     finish_b(0)
     finish_a(1)
+    x_finish(0)
+    x_finish(1)
+    x_finish(2)
     finish_b(1)
 
     def slot(i, r0=0, n=T):
@@ -671,7 +679,7 @@
     )
     g_copies[0].start()
     g_copies[1].start()
-    x_ring(6)[0]()
+    x_ring(6, 0)[0]()
 
     def h_copy(o):
         p = lax.rem(v + o, 16)
@@ -691,7 +699,9 @@
         h_copy(o).start()
         return carry
 
-    lax.fori_loop(1, 16, h_step, 0)
+    lax.fori_loop(1, 9, h_step, 0)
+    x_ring(6, 1)[0]()
+    lax.fori_loop(9, 16, h_step, 0)
     hrecv[0] = h_tile(0).astype(BF16)
     gpall[:, pl.ds(0, T)] = gpx[...]
     x_finish(3)
@@ -701,9 +711,10 @@
     g_copies[1].wait_recv()
     g_copies[3].start()
     x_ring(5)[1]()
-    x_ring(7)[0]()
+    x_ring(7, 0)[0]()
 
     rc(slot(3), slot(3), g_s, g_r.at[2], x_right).wait_recv()
+    x_ring(7, 1)[0]()
 
     def product(half, k):
         return nn(hst[pl.ds(pl.multiple_of(half * 256, 256), 256), :], gpall[k])
@@ -726,10 +737,14 @@
     )
     for cp in p_copies:
         cp.start()
-    x_ring(6)[1]()
+    x_ring(6, 0)[1]()
+    x_ring(6, 1)[1]()
     x_finish(5)
-    x_ring(7)[1]()
-    x_finish(6)
+    x_ring(7, 0)[1]()
+    x_finish(6, 0)
+    x_ring(7, 1)[1]()
+    x_finish(6, 1)
+    x_finish(7, 0)
     h_all = rc(hts.at[pl.ds(1, 15)], hrecv.at[pl.ds(1, 15)], h_s, h_r, partner_c)
     h_all.wait_recv()
     mw = jnp.concatenate(
@@ -745,7 +760,7 @@
         pltpu.make_async_copy(gm_v, gm_out, sem_o.at[2]),
     )
     out_copies[0].start()
-    x_finish(7)
+    x_finish(7, 1)
     for cp in p_copies:
         cp.wait_recv()
     for k in range(K):
@@ -757,7 +772,7 @@
     for cp in (info_copy, swap0, swap1, *p_copies, tl_all, hs_all, h_all, gm_all):
         cp.wait_send()
     for ref, sem in (
-        (comp.at[pl.ds(0, 992), :], ag_s),
+        (comp.at[pl.ds(0, 31)], ag_s),
         (part.at[pl.ds(0, 6)], x_s),
         (part.at[0], zx_s),
         (gcb.at[0, pl.ds(0, 3)], a_s),
@@ -807,7 +822,7 @@
             pltpu.VMEM((T, D), BF16),
             pltpu.VMEM((K, D, U), BF16),
             pltpu.VMEM((D, VH), BF16),
-            pltpu.VMEM((2 * R, D), BF16),
+            pltpu.VMEM((32, R, U), BF16),
             pltpu.VMEM((D, 2 * R), BF16),
             pltpu.VMEM((2 * R, VH), BF16),
             pltpu.VMEM((NC, 8, 256, C), BF16),
@@ -835,6 +850,7 @@
             pltpu.VMEM((2 * R, 128), F32),
             pltpu.VMEM((2 * R, 128), F32),
             pltpu.VMEM((32, 8, T), F32),
+            pltpu.VMEM((2 * K, T, U), F32),
             pltpu.VMEM((2 * R, W2), F32),
             pltpu.VMEM((T, U), BF16),
             pltpu.VMEM((K, 256), F32),
@@ -851,7 +867,7 @@
             dma,
             dma,
             dma,
-            dma((16,)),
+            dma((24,)),
             dma,
             dma,
             dma,

time: 117 us -> 114 us (0.974)
  Pallas kernels: 115 us -> 113 us
    pallas_call x1, Pallas kernels: 113 us -> 111 us  [shards(): pl.pallas_call(kernel, out_shape=outs, in_specs=[vm, vm, vm, vm, hbm, hbm...]
where the time goes in v4:
time: 114 us
  Pallas kernels  113 us (99%)
    pallas_call x1, Pallas kernels, shards(): pl.pallas_call(kernel, out_shape=outs, in_specs=[vm, vm, vm, vm, hbm, hbm...  111 us
    pallas_call x1, Pallas kernels, shards(): pl.pallas_call(place, out_shape=outs, in_specs=[hbm] * 4, out_specs=(hbm,...  2.57 us

profile of v4, /device:TPU:1, one launch (start us, length us, event | category | flops | bytes accessed | tf_op | source)
XLA Modules:
  0.0 114.0 jit_solution(17508261659088392826)
XLA Ops:
  0.6 110.6 %shard_map.102 = (bf16[128,128]{1,0:T(8,128)(2,1)}, f32[4,256]{1,0:T(4,128)}, bf16[4,256,128]{2,1,0:T(8,128)(2,1)}, bf16[256,4096]{1,0:T(8,128)(2,1)}) custom-call(bf16[4,2048]{1,0:T(4,128)(2,1)} %bitcast.5, f32[4,128]{1,0:T(4,128)} %bitcast.6, f32[1,128]{1,0:T(1,128)} %bitcast.7, s32[1,128]{1,0:T(1,128)} %bitcast.8, bf16[128,2048]{1,0:T(8,128)(2,1)} %hidden_hbm.1, ...), custom_call_target="tpu_custom_call" | custom-call | tf_op jit(solution)/shard_map/pallas_call | solution.py:816
  111.3 2.6 %shard_map.103 = (bf16[128,128]{1,0:T(8,128)(2,1)}, f32[4,256]{1,0:T(4,128)}, bf16[4,256,128]{2,1,0:T(8,128)(2,1)}, bf16[256,4096]{1,0:T(8,128)(2,1)}) custom-call(bf16[128,128]{1,0:T(8,128)(2,1)} %get-tuple-element.12.gh, f32[4,256]{1,0:T(4,128)} %get-tuple-element.13.gm, bf16[4,256,128]{2,1,0:T(8,128)(2,1)} %get-tuple-element.14.gp, ...), custom_call_target="tpu_custom_call" | custom-call | tf_op jit(solution)/shard_map/pallas_call | solution.py:899

commit v5 on v4

--- a/solution.py
+++ b/solution.py
@@ -36,10 +36,10 @@
 
 
 def kernel(
-    mix_t,
-    lse_t,
-    scale,
-    target,
+    mix_hbm,
+    lse_hbm,
+    scale_hbm,
+    target_hbm,
     hidden_hbm,
     proj_hbm,
     w_hbm,
@@ -47,6 +47,10 @@
     gm_out,
     gp_out,
     go_out,
+    mix_t,
+    lse_t,
+    scale,
+    target,
     hidden,
     proj,
     w,
@@ -147,9 +151,14 @@
     w_copy = pltpu.make_async_copy(
         w_hbm.at[:, pl.ds(pl.multiple_of(zl * VH, VH), VH)], w, sem_w.at[2]
     )
+    small_copies = [
+        pltpu.make_async_copy(src, dst, sem_w.at[3 + i])
+        for i, (src, dst) in enumerate(
+            ((mix_hbm, mix_t), (lse_hbm, lse_t), (scale_hbm, scale), (target_hbm, target))
+        )
+    ]
     hidden_copy.start()
     proj_copy.start()
-    w_copy.start()
 
     q32 = z * 8 + y * 2 + c
 
@@ -221,9 +230,12 @@
 
     hidden_copy.wait()
     proj_copy.wait()
+    for cp in small_copies:
+        cp.start()
+    w_copy.start()
+    pre = jnp.tanh(nn(hidden[...], jnp.concatenate([proj[k] for k in range(K)], axis=1)))
     for k in range(K):
-        pre = nn(hidden[...], proj[k])
-        comp[zl * 16 + v, pl.ds(k * T, T)] = jnp.tanh(pre).astype(BF16)
+        comp[zl * 16 + v, pl.ds(k * T, T)] = pre[:, k * U : (k + 1) * U].astype(BF16)
     pl.semaphore_wait(barrier, 34)
     for col in range(2):
         a, b = pos(col)
@@ -231,6 +243,8 @@
         ag_send(col, 0, own, dev_ab(col, m4(a + 1), b))
         ag_send(col, 1, own, dev_ab(col, m4(a - 1), b))
 
+    for cp in small_copies:
+        cp.wait()
     mix_logits = nt(mix_t[...], hidden[...])
     info2[zl, 0:4] = lse_t[...]
     info2[zl, 4:8] = mix_logits - jnp.log(jnp.sum(jnp.exp(mix_logits), axis=0, keepdims=True))
@@ -741,8 +755,8 @@
     x_ring(6, 1)[1]()
     x_finish(5)
     x_ring(7, 0)[1]()
+    x_ring(7, 1)[1]()
     x_finish(6, 0)
-    x_ring(7, 1)[1]()
     x_finish(6, 1)
     x_finish(7, 0)
     h_all = rc(hts.at[pl.ds(1, 15)], hrecv.at[pl.ds(1, 15)], h_s, h_r, partner_c)
@@ -789,8 +803,8 @@
 
 def place(gh, gm, gp, go, gh_o, gm_o, gp_o, go_o, b_gh, b_gm, b_gp, b_go, s_in, s_out):
     pairs = [(gh, b_gh, gh_o), (gm, b_gm, gm_o), (gp, b_gp, gp_o)]
-    for i in range(4):
-        rows = pl.ds(i * 64, 64)
+    for i in range(8):
+        rows = pl.ds(i * 32, 32)
         pairs.append((go.at[rows], b_go.at[rows], go_o.at[rows]))
     loads = [pltpu.make_async_copy(s, b, s_in.at[i]) for i, (s, b, _) in enumerate(pairs)]
     stores = [pltpu.make_async_copy(b, t, s_out.at[i]) for i, (_, b, t) in enumerate(pairs)]
@@ -804,7 +818,6 @@
 
 
 def shards(hidden, mix_weight, proj_weight, out_weight, saved_lse, targets, loss_scale):
-    vm = pl.BlockSpec(memory_space=pltpu.VMEM)
     hbm = pl.BlockSpec(memory_space=pltpu.HBM)
     dma = pltpu.SemaphoreType.DMA
     outs = (
@@ -816,9 +829,13 @@
     found = pl.pallas_call(
         kernel,
         out_shape=outs,
-        in_specs=[vm, vm, vm, vm, hbm, hbm, hbm],
+        in_specs=[hbm] * 7,
         out_specs=(hbm, hbm, hbm, hbm),
         scratch_shapes=[
+            pltpu.VMEM((K, D), BF16),
+            pltpu.VMEM((K, T), F32),
+            pltpu.VMEM((1, T), F32),
+            pltpu.VMEM((1, T), jnp.int32),
             pltpu.VMEM((T, D), BF16),
             pltpu.VMEM((K, D, U), BF16),
             pltpu.VMEM((D, VH), BF16),
@@ -855,7 +872,7 @@
             pltpu.VMEM((T, U), BF16),
             pltpu.VMEM((K, 256), F32),
             pltpu.VMEM((K, 256, U), BF16),
-            dma((3,)),
+            dma((7,)),
             dma((2,)),
             dma((2,)),
             dma((2,)),
@@ -901,7 +918,7 @@
         out_shape=outs,
         in_specs=[hbm] * 4,
         out_specs=(hbm,) * 4,
-        scratch_shapes=[pltpu.VMEM(o.shape, o.dtype) for o in outs] + [dma((7,)), dma((7,))],
+        scratch_shapes=[pltpu.VMEM(o.shape, o.dtype) for o in outs] + [dma((11,)), dma((11,))],
     )(*found)
     return gh, gm.T, gp, go
 

time: 114 us -> 114 us (level)
  no operation moved by 1% of the time
where the time goes in v5:
time: 114 us
  Pallas kernels  113 us (99%)
    pallas_call x1, Pallas kernels, shards(): pl.pallas_call(kernel, out_shape=outs, in_specs=[hbm] * 7, out_specs=(hbm...  110 us
    pallas_call x1, Pallas kernels, shards(): pl.pallas_call(place, out_shape=outs, in_specs=[hbm] * 4, out_specs=(hbm,...  2.55 us

profile of v5, /device:TPU:1, one launch (start us, length us, event | category | flops | bytes accessed | tf_op | source)
XLA Modules:
  0.0 113.5 jit_solution(1828245317438020640)
XLA Ops:
  0.6 110.2 %shard_map.102 = (bf16[128,128]{1,0:T(8,128)(2,1)}, f32[4,256]{1,0:T(4,128)}, bf16[4,256,128]{2,1,0:T(8,128)(2,1)}, bf16[256,4096]{1,0:T(8,128)(2,1)}) custom-call(bf16[4,2048]{1,0:T(4,128)(2,1)} %bitcast.5, f32[4,128]{1,0:T(4,128)} %bitcast.6, f32[1,128]{1,0:T(1,128)} %bitcast.7, s32[1,128]{1,0:T(1,128)} %bitcast.8, bf16[128,2048]{1,0:T(8,128)(2,1)} %hidden_hbm.1, ...), custom_call_target="tpu_custom_call" | custom-call | tf_op jit(solution)/shard_map/pallas_call | solution.py:829
  110.8 2.6 %shard_map.103 = (bf16[128,128]{1,0:T(8,128)(2,1)}, f32[4,256]{1,0:T(4,128)}, bf16[4,256,128]{2,1,0:T(8,128)(2,1)}, bf16[256,4096]{1,0:T(8,128)(2,1)}) custom-call(bf16[128,128]{1,0:T(8,128)(2,1)} %get-tuple-element.12.gh, f32[4,256]{1,0:T(4,128)} %get-tuple-element.13.gm, bf16[4,256,128]{2,1,0:T(8,128)(2,1)} %get-tuple-element.14.gp, ...), custom_call_target="tpu_custom_call" | custom-call | tf_op jit(solution)/shard_map/pallas_call | solution.py:916

commit v6 on v5

--- a/solution.py
+++ b/solution.py
@@ -100,6 +100,7 @@
     tl_r,
     x_s,
     x_r,
+    x_h,
     zx_s,
     zx_r,
     zx_l,
@@ -490,7 +491,7 @@
 
     def x_ring(cc, e=None):
         lanes = pl.ds(0, C) if e is None else pl.ds(e * 128, 128)
-        sem = 2 * cc if e is None else 2 * NC + 2 * (2 * (cc - 6) + e)
+        sem = 2 * cc if e is None else 2 * NC + 2 + 2 * e
         return ring(
             lambda t, h: part.at[cc, t * 2 + h, :, lanes],
             x,
@@ -648,6 +649,62 @@
         dst = go_out.at[:, cols]
         rc(part.at[cc, x * 2 + 1 - zl, :, lanes], dst, zx_s, zx_r, partner_z).start()
         pltpu.make_async_copy(part.at[cc, x * 2 + zl, :, lanes], dst, zx_l).start()
+
+    def last_ring(e):
+        lanes = pl.ds(e * 128, 128)
+        cc = NC - 1
+
+        def piece(t, h):
+            return part.at[cc, t * 2 + h, :, lanes]
+
+        def rf(i, h):
+            return rfx.at[cc, i, h, :, lanes]
+
+        def r1(i):
+            return r1x.at[cc, i, :, lanes]
+
+        def half(h):
+            return x_h.at[2 * e + h]
+
+        two, one, back = m4(x + 2), m4(x + 1), m4(x - 1)
+        leave, stay = m4(x + 1 - 2 * zl), m4(x - 1 + 2 * zl)
+        r1_all = r1x.at[cc, :, :, lanes]
+
+        def first():
+            rc(piece(two, 0), r1(0), x_s, x_r.at[2 * NC + e], x_right).start()
+            rc(piece(two, 1), r1(1), x_s, x_r.at[2 * NC + e], x_left).start()
+            rc(
+                piece(leave, 1 - zl), rf(zl, 1 - zl), x_s, half(1 - zl), dev(x_=leave)
+            ).start()
+
+        def forward():
+            rc(r1_all, r1_all, x_s, x_r.at[2 * NC + e], x_right).wait_recv()
+            for t, h in ((one, 0), (back, 1)):
+                ref = piece(t, h)
+                ref[...] = (ref[...].astype(F32) + r1(h)[...].astype(F32)).astype(BF16)
+                rc(ref, rf(h, h), x_s, half(h), dev(x_=t)).start()
+
+        def last():
+            rc(piece(stay, zl), rf(1 - zl, zl), x_s, half(zl), dev(x_=stay)).start()
+
+        def finish(h):
+            got = rfx.at[cc, :, h, :, lanes]
+            rc(got, got, x_s, half(h), x_right).wait_recv()
+            ref = piece(x, h)
+            ref[...] = (
+                ref[...].astype(F32) + rf(0, h)[...].astype(F32) + rf(1, h)[...].astype(F32)
+            ).astype(BF16)
+            return ref, go_out.at[:, pl.ds(pl.multiple_of(zl * VH + cc * C + e * 128, 128), 128)]
+
+        def cross():
+            ref, dst = finish(1 - zl)
+            rc(ref, dst, zx_s, zx_r, partner_z).start()
+
+        def keep():
+            ref, dst = finish(zl)
+            pltpu.make_async_copy(ref, dst, zx_l).start()
+
+        return first, forward, last, cross, keep
 
     first_half, second_half, every = range(4), range(4, 8), range(8)
     grad_out(0, every)
@@ -725,10 +782,10 @@
     g_copies[1].wait_recv()
     g_copies[3].start()
     x_ring(5)[1]()
-    x_ring(7, 0)[0]()
+    last_ring(0)[0]()
 
     rc(slot(3), slot(3), g_s, g_r.at[2], x_right).wait_recv()
-    x_ring(7, 1)[0]()
+    last_ring(1)[0]()
 
     def product(half, k):
         return nn(hst[pl.ds(pl.multiple_of(half * 256, 256), 256), :], gpall[k])
@@ -754,11 +811,14 @@
     x_ring(6, 0)[1]()
     x_ring(6, 1)[1]()
     x_finish(5)
-    x_ring(7, 0)[1]()
-    x_ring(7, 1)[1]()
+    last_ring(0)[1]()
+    last_ring(1)[1]()
+    last_ring(0)[2]()
+    last_ring(1)[2]()
     x_finish(6, 0)
     x_finish(6, 1)
-    x_finish(7, 0)
+    last_ring(0)[3]()
+    last_ring(1)[3]()
     h_all = rc(hts.at[pl.ds(1, 15)], hrecv.at[pl.ds(1, 15)], h_s, h_r, partner_c)
     h_all.wait_recv()
     mw = jnp.concatenate(
@@ -774,7 +834,8 @@
         pltpu.make_async_copy(gm_v, gm_out, sem_o.at[2]),
     )
     out_copies[0].start()
-    x_finish(7, 1)
+    last_ring(0)[4]()
+    last_ring(1)[4]()
     for cp in p_copies:
         cp.wait_recv()
     for k in range(K):
@@ -884,7 +945,8 @@
             dma,
             dma,
             dma,
-            dma((24,)),
+            dma((22,)),
+            dma((4,)),
             dma,
             dma,
             dma,

time: 114 us -> 113 us (level)
  no operation moved by 1% of the time
where the time goes in v6:
time: 113 us
  Pallas kernels  112 us (99%)
    pallas_call x1, Pallas kernels, shards(): pl.pallas_call(kernel, out_shape=outs, in_specs=[hbm] * 7, out_specs=(hbm...  109 us
    pallas_call x1, Pallas kernels, shards(): pl.pallas_call(place, out_shape=outs, in_specs=[hbm] * 4, out_specs=(hbm,...  2.55 us

profile of v6, /device:TPU:1, one launch (start us, length us, event | category | flops | bytes accessed | tf_op | source)
XLA Modules:
  0.0 112.6 jit_solution(6578448267166431485)
XLA Ops:
  0.6 109.3 %shard_map.102 = (bf16[128,128]{1,0:T(8,128)(2,1)}, f32[4,256]{1,0:T(4,128)}, bf16[4,256,128]{2,1,0:T(8,128)(2,1)}, bf16[256,4096]{1,0:T(8,128)(2,1)}) custom-call(bf16[4,2048]{1,0:T(4,128)(2,1)} %bitcast.5, f32[4,128]{1,0:T(4,128)} %bitcast.6, f32[1,128]{1,0:T(1,128)} %bitcast.7, s32[1,128]{1,0:T(1,128)} %bitcast.8, bf16[128,2048]{1,0:T(8,128)(2,1)} %hidden_hbm.1, ...), custom_call_target="tpu_custom_call" | custom-call | tf_op jit(solution)/shard_map/pallas_call | solution.py:890
  109.9 2.6 %shard_map.103 = (bf16[128,128]{1,0:T(8,128)(2,1)}, f32[4,256]{1,0:T(4,128)}, bf16[4,256,128]{2,1,0:T(8,128)(2,1)}, bf16[256,4096]{1,0:T(8,128)(2,1)}) custom-call(bf16[128,128]{1,0:T(8,128)(2,1)} %get-tuple-element.12.gh, f32[4,256]{1,0:T(4,128)} %get-tuple-element.13.gm, bf16[4,256,128]{2,1,0:T(8,128)(2,1)} %get-tuple-element.14.gp, ...), custom_call_target="tpu_custom_call" | custom-call | tf_op jit(solution)/shard_map/pallas_call | solution.py:978

commit v7 on v6

--- a/solution.py
+++ b/solution.py
@@ -785,6 +785,8 @@
     last_ring(0)[0]()
 
     rc(slot(3), slot(3), g_s, g_r.at[2], x_right).wait_recv()
+    x_ring(6, 0)[1]()
+    x_ring(6, 1)[1]()
     last_ring(1)[0]()
 
     def product(half, k):
@@ -808,8 +810,6 @@
     )
     for cp in p_copies:
         cp.start()
-    x_ring(6, 0)[1]()
-    x_ring(6, 1)[1]()
     x_finish(5)
     last_ring(0)[1]()
     last_ring(1)[1]()

time: 113 us -> 114 us (level)
  no operation moved by 1% of the time
where the time goes in v7:
time: 114 us; the launch traced here: 113 us
  Pallas kernels  112 us (98%)
    pallas_call x1, Pallas kernels, shards(): pl.pallas_call(kernel, out_shape=outs, in_specs=[hbm] * 7, out_specs=(hbm...  109 us
    pallas_call x1, Pallas kernels, shards(): pl.pallas_call(place, out_shape=outs, in_specs=[hbm] * 4, out_specs=(hbm,...  2.55 us

profile of v7, /device:TPU:1, one launch (start us, length us, event | category | flops | bytes accessed | tf_op | source)
XLA Modules:
  0.0 112.6 jit_solution(14446687722029967032)
XLA Ops:
  0.6 109.2 %shard_map.102 = (bf16[128,128]{1,0:T(8,128)(2,1)}, f32[4,256]{1,0:T(4,128)}, bf16[4,256,128]{2,1,0:T(8,128)(2,1)}, bf16[256,4096]{1,0:T(8,128)(2,1)}) custom-call(bf16[4,2048]{1,0:T(4,128)(2,1)} %bitcast.5, f32[4,128]{1,0:T(4,128)} %bitcast.6, f32[1,128]{1,0:T(1,128)} %bitcast.7, s32[1,128]{1,0:T(1,128)} %bitcast.8, bf16[128,2048]{1,0:T(8,128)(2,1)} %hidden_hbm.1, ...), custom_call_target="tpu_custom_call" | custom-call | tf_op jit(solution)/shard_map/pallas_call | solution.py:890
  109.8 2.6 %shard_map.103 = (bf16[128,128]{1,0:T(8,128)(2,1)}, f32[4,256]{1,0:T(4,128)}, bf16[4,256,128]{2,1,0:T(8,128)(2,1)}, bf16[256,4096]{1,0:T(8,128)(2,1)}) custom-call(bf16[128,128]{1,0:T(8,128)(2,1)} %get-tuple-element.12.gh, f32[4,256]{1,0:T(4,128)} %get-tuple-element.13.gm, bf16[4,256,128]{2,1,0:T(8,128)(2,1)} %get-tuple-element.14.gp, ...), custom_call_target="tpu_custom_call" | custom-call | tf_op jit(solution)/shard_map/pallas_call | solution.py:978
